TPU v7x, 256 devices: a whole 4x4x8 slice. The times are simulated.
256 devices in a mesh: seq: 32 (over x, y, core), tensor: 8 (over z).
Axes of the slice: x: 4, y: 4, z: 8, core: 2. Of those that a mesh axis runs over, the one named last changes fastest.
Arguments:
- queries: bfloat16 [32768, 8, 128], P('seq', 'tensor'), may hold values from -16 to 16
- keys: bfloat16 [32768, 128], P('seq'), may hold values from -6 to 6
- values: bfloat16 [32768, 128], P('seq'), may hold values from -6 to 6
- doc_ids: int32 [32768], P('seq'), may hold values from 0 to 31, never falling along the last dimension, each value on 1 to 4096 neighbouring positions
- w_query: bfloat16 [8, 128, 64], P('tensor'), may hold values from -0.5 to 0.5
- w_key: bfloat16 [128, 64], replicated, may hold values from -0.5 to 0.5
Outputs:
- student: bfloat16 [32768, 8, 128], P('seq', 'tensor')
- grad_wq: float32 [8, 128, 64], P('tensor')
- grad_key_weight: float32 [128, 64], replicated
- key_feature_grads: float32 [32768, 128], P('seq', 'tensor')
Inputs may be any that keep to these rules, and one draw needn't show every extreme that they name: `doc_ids`: document numbers never fall along the sequence and each number is used; each document has 1 to 4096 positions, and one has exactly 4096.
All inputs are finite; a program needn't handle non-finite values.
Results may differ from a plain program's by a relative error of at most 0.017.
Values may be sent and summed in bfloat16 or wider, within the bound.
A program may use at most 64 MiB of HBM per device.

v0:
```python
import jax
import jax.numpy as jnp
from jax import lax
from jax.sharding import Mesh
from jax.sharding import PartitionSpec as P

REACH = 4
SEQ = ("seq_0", "seq_1", "seq_2")


NEGATIVE = -1e30
exact_setting = lax.Precision.HIGHEST


def passed_along(block, axis, distance):
    devices = range(lax.axis_size(axis))
    route = [(i - distance, i) for i in devices if i - distance in devices]
    return lax.ppermute(block, axis, route)


def nothing_yet(array, identity):
    return jax.tree.map(
        lambda part, zero: jnp.zeros_like(part) + jnp.asarray(zero, part.dtype), array, identity
    )


def collected_together(array, axis):
    leaves = jax.tree.leaves(array)
    turns = sorted(range(len(leaves)), key=lambda k: -leaves[k].size)
    width = (1, *leaves[turns[0]].shape)[-1]
    lines = [
        jnp.pad(leaves[k].reshape(-1), (0, -leaves[k].size % width)).reshape(-1, width)
        for k in turns
    ]
    both, at, found = (lax.all_gather(jnp.concatenate(lines), axis), 0, {})
    for k, line in zip(turns, lines):
        section = both[:, at : at + len(line)].reshape(len(both), -1)
        found[k] = section[:, : leaves[k].size].reshape(-1, *leaves[k].shape)
        at += len(line)
    numbers = iter(range(len(leaves)))
    return jax.tree.map(lambda _: found[next(numbers)], array)


def carried_in(array, axes, combine, identity):
    before = start = nothing_yet(array, identity)
    so_far = array
    for axis in reversed(axes):
        size, index = (lax.axis_size(axis), lax.axis_index(axis))
        pieces = collected_together(
            jax.tree.map(
                lambda part, kind: part.astype(kind),
                so_far,
                (jnp.bfloat16, jnp.bfloat16, jnp.bfloat16),
            ),
            axis,
        )
        inside, so_far = (start, start)
        for k in range(size):
            passed = k < index
            so_far = combine(
                so_far, jax.tree.map(lambda part, own: part[k].astype(own.dtype), pieces, array)
            )
            inside = jax.tree.map(lambda new, old: jnp.where(passed, new, old), so_far, inside)
        before = combine(inside, before)
    return before


def once_a_type(array, axis):
    leaves, found = (jax.tree.leaves(array), {})
    for initial, a in enumerate(leaves):
        if initial not in found:
            alike = [k for k, b in enumerate(leaves) if b.dtype == a.dtype]
            got = (
                collected_together([leaves[k] for k in alike], axis)
                if len(alike) > 1
                else [lax.all_gather(a, axis)]
            )
            for k, b in zip(alike, got):
                found[k] = b
    numbers = iter(range(len(leaves)))
    return jax.tree.map(lambda _: found[next(numbers)], array)


def carried_in_2(array, axes, combine, identity):
    before = start = nothing_yet(array, identity)
    so_far = array
    for axis in reversed(axes):
        size, index = (lax.axis_size(axis), lax.axis_index(axis))
        pieces = once_a_type(
            jax.tree.map(
                lambda part, kind: part.astype(kind),
                so_far,
                jax.tree.map(lambda a: jnp.bfloat16 if a.dtype == jnp.float32 else a.dtype, array),
            ),
            axis,
        )
        inside, so_far = (start, start)
        for k in reversed(range(size)):
            passed = k > index
            so_far = combine(
                so_far, jax.tree.map(lambda part, own: part[k].astype(own.dtype), pieces, array)
            )
            inside = jax.tree.map(lambda new, old: jnp.where(passed, new, old), so_far, inside)
        before = combine(inside, before)
    return before


def in_blocks(array, dim, size):
    before, after = (array.shape[:dim], array.shape[dim + 1 :])
    return jnp.moveaxis(array.reshape(*before, size, -1, *after), dim, 0)


def sum_at_owner(array, axis, dim):
    parts = in_blocks(array, dim, lax.axis_size(axis))
    arrived = lax.all_to_all(parts, axis, split_axis=0, concat_axis=0, tiled=True)
    return arrived.astype(jnp.float32).sum(axis=0)


def sent_to_all(array, axis):
    size = lax.axis_size(axis)
    return lax.all_to_all(
        jnp.broadcast_to(array[None], (size, *array.shape)), axis, 0, 0, tiled=True
    )


def over_copies(array, axis):
    return sent_to_all(array, axis).astype(jnp.float32).sum(axis=0)


def feature(logits):
    return jnp.concatenate(
        [jax.nn.softmax(logits, axis=-1), jax.nn.softmax(-logits, axis=-1)], axis=-1
    )


def feature_back(features, incoming_grad):
    middle = features.shape[-1] // 2
    upper_half = features[..., :middle]
    lower_half = features[..., middle:]
    grad_upper = incoming_grad[..., :middle]
    grad_lower = incoming_grad[..., middle:]
    upper_term = upper_half * (
        grad_upper - jnp.sum(grad_upper * upper_half, axis=-1, keepdims=True)
    )
    lower_term = lower_half * (
        grad_lower - jnp.sum(grad_lower * lower_half, axis=-1, keepdims=True)
    )
    return upper_term - lower_term


def join_states(earlier, later):
    earlier_state, earlier_sum, earlier_code = earlier
    later_state, later_sum, later_code = later
    vacant = later_code == 0.0
    matching = (later_code == earlier_code).astype(jnp.float32)
    joined_state = jnp.where(vacant, earlier_state, later_state + matching * earlier_state)
    joined_sum = jnp.where(vacant, earlier_sum, later_sum + matching * earlier_sum)
    return (joined_state, joined_sum, jnp.where(vacant, earlier_code, later_code))


def tile_update(
    running, query_rows, query_codes, key_rows, value_rows, key_codes, causal, score_scale
):
    row_top, weight_sum, accumulated = running
    scores = (
        jnp.einsum("qhd,kd->qhk", query_rows, key_rows, preferred_element_type=jnp.float32)
        * score_scale
    )
    allowed = query_codes[:, None] == key_codes[None, :]
    if causal is not None:
        allowed = allowed & causal
    new_top = jnp.maximum(
        row_top, jnp.max(jnp.where(allowed[:, None, :], scores, NEGATIVE), axis=-1)
    )
    weights = jnp.where(allowed[:, None, :], jnp.exp(scores - new_top[..., None]), 0.0)
    factor = jnp.exp(row_top - new_top)
    weight_sum = weight_sum * factor + jnp.sum(weights, axis=-1)
    accumulated = accumulated * factor[..., None] + jnp.einsum(
        "qhk,kd->qhd", weights.astype(jnp.bfloat16), value_rows, preferred_element_type=jnp.float32
    )
    return (new_top, weight_sum, accumulated)


def shards(queries, keys, values, doc_ids, w_query, w_key):
    count_of_rows, head_count, head_width = queries.shape
    score_scale = head_width ** (-0.5)
    seq_devices = lax.axis_size(SEQ)
    grad_scale = 2.0 / (count_of_rows * seq_devices)
    step_rows = min(count_of_rows, 512)
    doc_codes = (doc_ids + 1).astype(jnp.float32)
    code_wire = doc_codes.astype(jnp.bfloat16)
    window = []
    for distance in range(1, REACH + 1):
        window.append(passed_along((keys, values, code_wire), SEQ, distance))
    key_features = feature(jnp.dot(keys, w_key, preferred_element_type=jnp.float32))
    key_feat_b = key_features.astype(jnp.bfloat16)
    feature_count = key_features.shape[1]
    chosen = (doc_codes == doc_codes[-1]).astype(jnp.bfloat16)[:, None] * key_feat_b
    state_local = jnp.einsum("kf,kd->fd", chosen, values, preferred_element_type=jnp.float32)
    sum_local = jnp.sum(chosen.astype(jnp.float32), axis=0)
    code_last = doc_codes[-1]
    identity = (
        jnp.zeros((feature_count, head_width), jnp.float32),
        jnp.zeros((feature_count,), jnp.float32),
        jnp.zeros((), jnp.float32),
    )
    incoming = carried_in((state_local, sum_local, code_last), SEQ, join_states, identity)
    carried_state, carried_sum, carried_code = incoming
    grad_kf = jnp.zeros((count_of_rows, feature_count), jnp.float32)
    grad_wq_local = jnp.zeros(w_query.shape, jnp.float32)
    adjoint_state = jnp.zeros((feature_count, head_width), jnp.float32)
    adjoint_sum = jnp.zeros((feature_count,), jnp.float32)
    leading_code = doc_codes[0]
    student_parts = []
    for block_index in range(count_of_rows // step_rows):
        first_row = block_index * step_rows
        key_limit = first_row + step_rows
        query_rows = queries[first_row:key_limit]
        query_codes = doc_codes[first_row:key_limit]
        causal = jnp.arange(key_limit)[None, :] <= (first_row + jnp.arange(step_rows))[:, None]
        running = (
            jnp.full((step_rows, head_count), NEGATIVE, jnp.float32),
            jnp.zeros((step_rows, head_count), jnp.float32),
            jnp.zeros((step_rows, head_count, head_width), jnp.float32),
        )
        running = tile_update(
            running,
            query_rows,
            query_codes,
            keys[:key_limit],
            values[:key_limit],
            doc_codes[:key_limit],
            causal,
            score_scale,
        )
        for window_piece in window:
            piece_codes = window_piece[2].astype(jnp.float32)

            def far_update(
                current,
                window_piece=window_piece,
                piece_codes=piece_codes,
                query_rows=query_rows,
                query_codes=query_codes,
            ):
                return tile_update(
                    current,
                    query_rows,
                    query_codes,
                    window_piece[0],
                    window_piece[1],
                    piece_codes,
                    None,
                    score_scale,
                )

            running = lax.cond(
                piece_codes[-1] == query_codes[0], far_update, lambda current: current, running
            )
        teacher = running[2] / running[1][..., None]
        query_features = feature(
            jnp.einsum("qhd,hdf->qhf", query_rows, w_query, preferred_element_type=jnp.float32)
        )
        query_feat_b = query_features.astype(jnp.bfloat16)
        query_feat_f = query_feat_b.astype(jnp.float32)
        allowed = (query_codes[:, None] == doc_codes[None, :key_limit]) & causal
        products = jnp.where(
            allowed[:, None, :],
            jnp.einsum(
                "qhf,kf->qhk",
                query_feat_b,
                key_feat_b[:key_limit],
                preferred_element_type=jnp.float32,
            ),
            0.0,
        )
        receive = (query_codes == carried_code).astype(jnp.float32)
        numerator = jnp.einsum(
            "qhk,kd->qhd",
            products.astype(jnp.bfloat16),
            values[:key_limit],
            preferred_element_type=jnp.float32,
        ) + receive[:, None, None] * jnp.einsum(
            "qhf,fd->qhd", query_feat_f, carried_state, precision=exact_setting
        )
        denominator = jnp.sum(products, axis=-1) + receive[:, None] * jnp.einsum(
            "qhf,f->qh", query_feat_f, carried_sum, precision=exact_setting
        )
        estimate = numerator / denominator[..., None]
        student_parts.append(estimate.astype(jnp.bfloat16))
        grad_out = grad_scale * (estimate - teacher)
        grad_num = grad_out / denominator[..., None]
        grad_den = -jnp.sum(grad_out * estimate, axis=-1) / denominator
        grad_prod = jnp.where(
            allowed[:, None, :],
            jnp.einsum(
                "qhd,kd->qhk",
                grad_num.astype(jnp.bfloat16),
                values[:key_limit],
                preferred_element_type=jnp.float32,
            )
            + grad_den[..., None],
            0.0,
        ).astype(jnp.bfloat16)
        grad_qf = jnp.einsum(
            "qhk,kf->qhf", grad_prod, key_feat_b[:key_limit], preferred_element_type=jnp.float32
        ) + receive[:, None, None] * (
            jnp.einsum("qhd,fd->qhf", grad_num, carried_state, precision=exact_setting)
            + grad_den[..., None] * carried_sum
        )
        grad_kf = grad_kf.at[:key_limit].add(
            jnp.einsum("qhk,qhf->kf", grad_prod, query_feat_b, preferred_element_type=jnp.float32)
        )
        leading = (query_codes == leading_code).astype(jnp.float32)[:, None, None] * query_feat_f
        adjoint_state = adjoint_state + jnp.einsum(
            "qhf,qhd->fd", leading, grad_num, precision=exact_setting
        )
        adjoint_sum = adjoint_sum + jnp.einsum(
            "qhf,qh->f", leading, grad_den, precision=exact_setting
        )
        grad_aq = feature_back(query_features, grad_qf).astype(jnp.bfloat16)
        grad_wq_local = grad_wq_local + jnp.einsum(
            "qhd,qhf->hdf", query_rows, grad_aq, preferred_element_type=jnp.float32
        )
    adjoint_entering = carried_in_2(
        (adjoint_state, adjoint_sum, leading_code), SEQ, join_states, identity
    )
    receive_back = (doc_codes == adjoint_entering[2]).astype(jnp.float32)
    additional_terms = (
        jnp.einsum(
            "kd,fd->kf", values.astype(jnp.float32), adjoint_entering[0], precision=exact_setting
        )
        + adjoint_entering[1][None, :]
    )
    grad_kf = grad_kf + receive_back[:, None] * additional_terms
    grad_attention_key = feature_back(key_features, grad_kf).astype(jnp.bfloat16)
    grad_wk_local = jnp.einsum(
        "kd,kf->df", keys, grad_attention_key, preferred_element_type=jnp.float32
    )
    key_feature_grads = sum_at_owner(
        (grad_kf * float(count_of_rows * seq_devices)).astype(jnp.bfloat16), "tensor", 1
    )
    grad_wq, partial_wk = (
        over_copies(grad_wq_local.astype(jnp.bfloat16), SEQ).astype(jnp.float32),
        over_copies(grad_wk_local.astype(jnp.bfloat16), SEQ).astype(jnp.float32),
    )
    grad_key_weight = over_copies(partial_wk.astype(jnp.bfloat16), "tensor").astype(jnp.float32)
    student = jnp.concatenate(student_parts, axis=0)
    return (student, grad_wq, grad_key_weight, key_feature_grads)


def solution(mesh):
    torus = Mesh(
        mesh.devices.reshape(4, 4, 2, mesh.shape["tensor"]), ("seq_0", "seq_1", "seq_2", "tensor")
    )
    placed = (
        P(SEQ, "tensor", None),
        P(SEQ, None),
        P(SEQ, None),
        P(SEQ),
        P("tensor", None, None),
        P(),
    )
    return jax.shard_map(
        shards,
        mesh=torus,
        in_specs=placed,
        out_specs=(P(SEQ, "tensor", None), P("tensor", None, None), P(), P(SEQ, "tensor")),
        check_vma=False,
    )
```

profile of v0, /device:TPU:1, one launch (start us, length us, event | category | flops | bytes accessed | tf_op | source)
XLA Modules:
  0.0 273.2 jit_solution(11093049530941117811)
XLA Ops:
  1.3 4.6 %collective-permute-start.3 = (bf16[1024]{0:T(1024)(128)(2,1)S(1)}, bf16[1024]{0:T(1024)(128)(2,1)S(1)}, u32[]{:S(2)}, u32[]{:S(2)}) collective-permute-start(bf16[1024]{0:T(1024)(128)(2,1)S(1)} %get-tuple-element.411), channel_id=1, source_target_pairs={{0,8},{8,16},{16,24},{24,32},{32,40},{40,48},{48,56},{56,64},{64,7... | collective-permute-start | bytes 6152 | tf_op jit(solution)/shard_map/ppermute | solution.py:18
  5.9 3.2 %collective-permute-start.2 = (bf16[1024]{0:T(1024)(128)(2,1)S(1)}, bf16[1024]{0:T(1024)(128)(2,1)S(1)}, u32[]{:S(2)}, u32[]{:S(2)}) collective-permute-start(bf16[1024]{0:T(1024)(128)(2,1)S(1)} %get-tuple-element.411), channel_id=1, source_target_pairs={{0,16},{8,24},{16,32},{24,40},{32,48},{40,56},{48,64},{56,72},{64,... | collective-permute-start | bytes 6152 | tf_op jit(solution)/shard_map/ppermute | solution.py:18
  9.1 3.6 %collective-permute-start.6 = (bf16[1024,128]{1,0:T(8,128)(2,1)}, bf16[1024,128]{1,0:T(8,128)(2,1)}, u32[]{:S(2)}, u32[]{:S(2)}) collective-permute-start(bf16[1024,128]{1,0:T(8,128)(2,1)} %param.29), channel_id=1, source_target_pairs={{0,16},{8,24},{16,32},{24,40},{32,48},{40,56},{48,64},{56,72},{64,... | collective-permute-start | bytes 786440 | tf_op jit(solution)/shard_map/ppermute | solution.py:18
  12.7 1.9 collective-permute-start.4
  14.7 2.5 collective-permute-start.5
  25.9 2.1 all-gather.6
  32.0 9.8 %all-gather.7 = bf16[4,130,128]{2,1,0:T(8,128)(2,1)S(1)} all-gather(bf16[1,130,128]{2,1,0:T(8,128)(2,1)S(1)} %maximum_bitcast_fusion.1), channel_id=3, replica_groups=mesh['seq_0'=4,'seq_1'=4,'seq_2'=2,'tensor'=8] {'seq_1'}, dimensions={0}, use_global_device_ids=true | all-gather | bytes 166400 | tf_op jit(solution)/shard_map/all_gather | solution.py:35
  49.8 9.2 %all-gather.8 = bf16[4,130,128]{2,1,0:T(8,128)(2,1)S(1)} all-gather(bf16[1,130,128]{2,1,0:T(8,128)(2,1)S(1)} %maximum_bitcast_fusion.2), channel_id=4, replica_groups=mesh['seq_0'=4,'seq_1'=4,'seq_2'=2,'tensor'=8] {'seq_0'}, dimensions={0}, use_global_device_ids=true | all-gather | bytes 166400 | tf_op jit(solution)/shard_map/all_gather | solution.py:35
  72.3 1.7 fusion.122
  74.1 2.3 fusion.130
  77.9 8.4 %collective-permute-start.1 = (bf16[1024]{0:T(1024)(128)(2,1)S(1)}, bf16[1024]{0:T(1024)(128)(2,1)S(1)}, u32[]{:S(2)}, u32[]{:S(2)}) collective-permute-start(bf16[1024]{0:T(1024)(128)(2,1)S(1)} %get-tuple-element.411), channel_id=1, source_target_pairs={{0,24},{8,32},{16,40},{24,48},{32,56},{40,64},{48,72},{56,80},{64,... | collective-permute-start | bytes 6152 | tf_op jit(solution)/shard_map/ppermute | solution.py:18
  86.3 3.8 %collective-permute-start = (bf16[1024]{0:T(1024)(128)(2,1)S(1)}, bf16[1024]{0:T(1024)(128)(2,1)S(1)}, u32[]{:S(2)}, u32[]{:S(2)}) collective-permute-start(bf16[1024]{0:T(1024)(128)(2,1)S(1)} %get-tuple-element.411), channel_id=1, source_target_pairs={{0,32},{8,40},{16,48},{24,56},{32,64},{40,72},{48,80},{56,88},{64,... | collective-permute-start | bytes 6152 | tf_op jit(solution)/shard_map/ppermute | solution.py:18
  92.1 3.8 %collective-permute-start.10 = (bf16[1024,128]{1,0:T(8,128)(2,1)S(1)}, bf16[1024,128]{1,0:T(8,128)(2,1)}, u32[]{:S(2)}, u32[]{:S(2)}) collective-permute-start(bf16[1024,128]{1,0:T(8,128)(2,1)S(1)} %copy-done.10), channel_id=1, source_target_pairs={{0,32},{8,40},{16,48},{24,56},{32,64},{40,72},{48,80},{56,88},{64,... | collective-permute-start | bytes 786440 | tf_op jit(solution)/shard_map/ppermute | solution.py:18
  95.9 2.5 collective-permute-start.8
  98.4 3.9 %collective-permute-start.11 = (bf16[1024,128]{1,0:T(8,128)(2,1)}, bf16[1024,128]{1,0:T(8,128)(2,1)}, u32[]{:S(2)}, u32[]{:S(2)}) collective-permute-start(bf16[1024,128]{1,0:T(8,128)(2,1)} %param.30), channel_id=1, source_target_pairs={{0,32},{8,40},{16,48},{24,56},{32,64},{40,72},{48,80},{56,88},{64,... | collective-permute-start | bytes 786440 | tf_op jit(solution)/shard_map/ppermute | solution.py:18
  102.4 4.9 %collective-permute-start.9 = (bf16[1024,128]{1,0:T(8,128)(2,1)}, bf16[1024,128]{1,0:T(8,128)(2,1)}, u32[]{:S(2)}, u32[]{:S(2)}) collective-permute-start(bf16[1024,128]{1,0:T(8,128)(2,1)} %param.30), channel_id=1, source_target_pairs={{0,24},{8,32},{16,40},{24,48},{32,56},{40,64},{48,72},{56,80},{64,... | collective-permute-start | bytes 786440 | tf_op jit(solution)/shard_map/ppermute | solution.py:18
  107.2 2.9 %collective-permute-start.7 = (bf16[1024,128]{1,0:T(8,128)(2,1)}, bf16[1024,128]{1,0:T(8,128)(2,1)}, u32[]{:S(2)}, u32[]{:S(2)}) collective-permute-start(bf16[1024,128]{1,0:T(8,128)(2,1)} %param.30), channel_id=1, source_target_pairs={{0,16},{8,24},{16,32},{24,40},{32,48},{40,56},{48,64},{56,72},{64,... | collective-permute-start | bytes 786440 | tf_op jit(solution)/shard_map/ppermute | solution.py:18
  124.3 3.8 %conditional.8 = ((f32[512,1]{0,1:T(1,128)S(1)}, f32[512,1]{0,1:T(1,128)S(1)}, f32[512,1,128]{2,0,1:T(8,128)S(1)})) conditional(s32[]{:T(128)} %convert_element_type.1073, (f32[512,1]{0,1:T(1,128)S(1)}, f32[512,1]{0,1:T(1,128)S(1)}, f32[512,1,128]{2,0,1:T(8,128)S(1)}) %tuple.192, (f32[512]{0:T(512)S(1)}, f32[1024]{0:T(1024)S(1)}, ...), branch_computations={%region_17.18_spmd, %region_18.21_spmd} | conditional | flops 275907584 | bytes 7522336 | solution.py:257
  126.5 1.6 fusion.3
  130.7 1.9 all-gather.9
  136.2 26.7 %all-gather.10 = bf16[4,130,128]{2,1,0:T(8,128)(2,1)S(1)} all-gather(bf16[1,130,128]{2,1,0:T(8,128)(2,1)S(1)} %maximum_bitcast_fusion.4), channel_id=6, replica_groups=mesh['seq_0'=4,'seq_1'=4,'seq_2'=2,'tensor'=8] {'seq_1'}, dimensions={0}, use_global_device_ids=true | all-gather | bytes 166400 | tf_op jit(solution)/shard_map/all_gather | solution.py:35
  173.0 1.7 select_convert_fusion
  175.5 9.1 %all-gather.11 = bf16[4,130,128]{2,1,0:T(8,128)(2,1)S(1)} all-gather(bf16[1,130,128]{2,1,0:T(8,128)(2,1)S(1)} %maximum_bitcast_fusion.5), channel_id=7, replica_groups=mesh['seq_0'=4,'seq_1'=4,'seq_2'=2,'tensor'=8] {'seq_0'}, dimensions={0}, use_global_device_ids=true | all-gather | bytes 166400 | tf_op jit(solution)/shard_map/all_gather | solution.py:35
  198.6 1.6 fusion.111
  201.3 8.3 %all-to-all-start.3 = ((bf16[8,1024,16]{1,2,0:T(8,128)(2,1)}), bf16[8,1024,16]{1,2,0:T(8,128)(2,1)S(1)}, u32[]{:S(2)}, u32[]{:S(2)}) async-start(bf16[8,1024,16]{1,2,0:T(8,128)(2,1)} %bitcast.993), calls=%async_computation.3 | async-start | bytes 524288 | tf_op jit(solution)/shard_map/all_to_all | solution.py:115
  212.3 6.7 %all-to-all-done.3 = bf16[8,1024,16]{1,2,0:T(8,128)(2,1)S(1)} async-done(((bf16[8,1024,16]{1,2,0:T(8,128)(2,1)}), bf16[8,1024,16]{1,2,0:T(8,128)(2,1)S(1)}, u32[]{:S(2)}, u32[]{:S(2)}) %all-to-all-start.3) | async-done | bytes 262176 | tf_op jit(solution)/shard_map/all_to_all | solution.py:115
  219.9 11.3 %all-to-all-start.1 = ((bf16[32,128,64]{1,2,0:T(8,128)(2,1)}), bf16[32,128,64]{1,2,0:T(8,128)(2,1)S(1)}, u32[]{:S(2)}, u32[]{:S(2)}) async-start(bf16[32,128,64]{1,2,0:T(8,128)(2,1)} %broadcast_in_dim.125), calls=%async_computation.1 | async-start | bytes 1048576 | tf_op jit(solution)/shard_map/all_to_all | solution.py:121
  231.8 11.0 %all-to-all-done.1 = bf16[32,128,64]{1,2,0:T(8,128)(2,1)S(1)} async-done(((bf16[32,128,64]{1,2,0:T(8,128)(2,1)}), bf16[32,128,64]{1,2,0:T(8,128)(2,1)S(1)}, u32[]{:S(2)}, u32[]{:S(2)}) %all-to-all-start.1) | async-done | bytes 524320 | tf_op jit(solution)/shard_map/all_to_all | solution.py:121
  243.7 3.7 %all-to-all-start = ((bf16[32,1,128,64]{2,3,1,0:T(8,128)(2,1)}), bf16[32,1,128,64]{2,3,1,0:T(8,128)(2,1)S(1)}, u32[]{:S(2)}, u32[]{:S(2)}) async-start(bf16[32,1,128,64]{2,3,1,0:T(8,128)(2,1)} %broadcast_in_dim.124), calls=%async_computation | async-start | bytes 1048576 | tf_op jit(solution)/shard_map/all_to_all | solution.py:121
  248.4 10.5 %all-to-all-done = bf16[32,1,128,64]{2,3,1,0:T(8,128)(2,1)S(1)} async-done(((bf16[32,1,128,64]{2,3,1,0:T(8,128)(2,1)}), bf16[32,1,128,64]{2,3,1,0:T(8,128)(2,1)S(1)}, u32[]{:S(2)}, u32[]{:S(2)}) %all-to-all-start) | async-done | bytes 524320 | tf_op jit(solution)/shard_map/all_to_all | solution.py:121
  259.6 3.4 %all-to-all-start.2 = ((bf16[8,128,64]{1,2,0:T(8,128)(2,1)}), bf16[8,128,64]{1,2,0:T(8,128)(2,1)S(1)}, u32[]{:S(2)}, u32[]{:S(2)}) async-start(bf16[8,128,64]{1,2,0:T(8,128)(2,1)} %broadcast_in_dim.132), calls=%async_computation.2 | async-start | bytes 262144 | tf_op jit(solution)/shard_map/all_to_all | solution.py:121
  264.4 8.2 %all-to-all-done.2 = bf16[8,128,64]{1,2,0:T(8,128)(2,1)S(1)} async-done(((bf16[8,128,64]{1,2,0:T(8,128)(2,1)}), bf16[8,128,64]{1,2,0:T(8,128)(2,1)S(1)}, u32[]{:S(2)}, u32[]{:S(2)}) %all-to-all-start.2) | async-done | bytes 131104 | tf_op jit(solution)/shard_map/all_to_all | solution.py:121
  (249 shorter events, 48.2 us)
Async XLA Ops:
  1.3 75.1 %copy-start.20 = (f32[1024]{0:T(1024)}, f32[1024]{0:T(1024)S(1)}, u32[]{:S(2)}) copy-start(f32[1024]{0:T(1024)S(1)} %get-tuple-element.412) | copy-start | bytes 12292
  1.3 76.5 %collective-permute-start.3 = (bf16[1024]{0:T(1024)(128)(2,1)S(1)}, bf16[1024]{0:T(1024)(128)(2,1)S(1)}, u32[]{:S(2)}, u32[]{:S(2)}) collective-permute-start(bf16[1024]{0:T(1024)(128)(2,1)S(1)} %get-tuple-element.411), channel_id=1, source_target_pairs={{0,8},{8,16},{16,24},{24,32},{32,40},{40,48},{48,56},{56,64},{64,7... | collective-permute-start | bytes 6152 | tf_op jit(solution)/shard_map/ppermute | solution.py:18
  5.9 80.4 %collective-permute-start.2 = (bf16[1024]{0:T(1024)(128)(2,1)S(1)}, bf16[1024]{0:T(1024)(128)(2,1)S(1)}, u32[]{:S(2)}, u32[]{:S(2)}) collective-permute-start(bf16[1024]{0:T(1024)(128)(2,1)S(1)} %get-tuple-element.411), channel_id=1, source_target_pairs={{0,16},{8,24},{16,32},{24,40},{32,48},{40,56},{48,64},{56,72},{64,... | collective-permute-start | bytes 6152 | tf_op jit(solution)/shard_map/ppermute | solution.py:18
  9.1 89.3 %collective-permute-start.6 = (bf16[1024,128]{1,0:T(8,128)(2,1)}, bf16[1024,128]{1,0:T(8,128)(2,1)}, u32[]{:S(2)}, u32[]{:S(2)}) collective-permute-start(bf16[1024,128]{1,0:T(8,128)(2,1)} %param.29), channel_id=1, source_target_pairs={{0,16},{8,24},{16,32},{24,40},{32,48},{40,56},{48,64},{56,72},{64,... | collective-permute-start | bytes 786440 | tf_op jit(solution)/shard_map/ppermute | solution.py:18
  12.7 89.6 %collective-permute-start.4 = (bf16[1024,128]{1,0:T(8,128)(2,1)}, bf16[1024,128]{1,0:T(8,128)(2,1)}, u32[]{:S(2)}, u32[]{:S(2)}) collective-permute-start(bf16[1024,128]{1,0:T(8,128)(2,1)} %param.29), channel_id=1, source_target_pairs={{0,8},{8,16},{16,24},{24,32},{32,40},{40,48},{48,56},{56,64},{64,7... | collective-permute-start | bytes 786440 | tf_op jit(solution)/shard_map/ppermute | solution.py:18
  14.7 92.6 %collective-permute-start.5 = (bf16[1024,128]{1,0:T(8,128)(2,1)}, bf16[1024,128]{1,0:T(8,128)(2,1)}, u32[]{:S(2)}, u32[]{:S(2)}) collective-permute-start(bf16[1024,128]{1,0:T(8,128)(2,1)} %param.30), channel_id=1, source_target_pairs={{0,8},{8,16},{16,24},{24,32},{32,40},{40,48},{48,56},{56,64},{64,7... | collective-permute-start | bytes 786440 | tf_op jit(solution)/shard_map/ppermute | solution.py:18
  17.2 56.9 %copy-start.51 = (s32[512]{0:T(512)}, s32[512]{0:T(512)S(1)}, u32[]{:S(2)}) copy-start(s32[512]{0:T(512)S(1)} %iota_add_fusion) | copy-start | bytes 6148
  19.8 108.6 %copy-start.13 = (f32[512]{0:T(512)}, f32[512]{0:T(512)S(1)}, u32[]{:S(2)}) copy-start(f32[512]{0:T(512)S(1)} %get-tuple-element.415) | copy-start | bytes 6148
  19.8 108.9 %copy-start.19 = (f32[512]{0:T(512)}, f32[512]{0:T(512)S(1)}, u32[]{:S(2)}) copy-start(f32[512]{0:T(512)S(1)} %get-tuple-element.416) | copy-start | bytes 6148
  20.9 50.0 %copy-start.25 = (f32[512]{0:T(512)}, f32[512]{0:T(512)S(1)}, u32[]{:S(2)}) copy-start(f32[512]{0:T(512)S(1)} %get-tuple-element.444) | copy-start | bytes 6148
  22.0 46.2 %copy-start.27 = (f32[512]{0:T(512)}, f32[512]{0:T(512)S(1)}, u32[]{:S(2)}) copy-start(f32[512]{0:T(512)S(1)} %get-tuple-element.447) | copy-start | bytes 6148
  23.0 44.7 %copy-start.1 = (bf16[1024,1,128]{2,0,1:T(8,128)(2,1)S(1)}, bf16[1024,1,128]{2,0,1:T(8,128)(2,1)}, u32[]{:S(2)}) copy-start(bf16[1024,1,128]{2,0,1:T(8,128)(2,1)} %param.28) | copy-start | bytes 786436
  23.1 44.7 %copy-start.10 = (bf16[1024,128]{1,0:T(8,128)(2,1)S(1)}, bf16[1024,128]{1,0:T(8,128)(2,1)}, u32[]{:S(2)}) copy-start(bf16[1024,128]{1,0:T(8,128)(2,1)} %param.29) | copy-start | bytes 786436
  24.3 43.8 %copy-start.15 = (f32[1024]{0:T(1024)}, f32[1024]{0:T(1024)S(1)}, u32[]{:S(2)}) copy-start(f32[1024]{0:T(1024)S(1)} %get-tuple-element.342) | copy-start | bytes 12292
  68.3 61.2 %copy-start.5 = (bf16[512,64]{0,1:T(8,128)(2,1)}, bf16[512,64]{0,1:T(8,128)(2,1)S(1)}, u32[]{:S(2)}) copy-start(bf16[512,64]{0,1:T(8,128)(2,1)S(1)} %get-tuple-element.404) | copy-start | bytes 196612
  71.0 58.2 %copy-start.6 = (bf16[512,64]{0,1:T(8,128)(2,1)}, bf16[512,64]{0,1:T(8,128)(2,1)S(1)}, u32[]{:S(2)}) copy-start(bf16[512,64]{0,1:T(8,128)(2,1)S(1)} %get-tuple-element.395) | copy-start | bytes 196612
  71.0 58.2 %copy-start.8 = (bf16[512,64]{0,1:T(8,128)(2,1)}, bf16[512,64]{0,1:T(8,128)(2,1)S(1)}, u32[]{:S(2)}) copy-start(bf16[512,64]{0,1:T(8,128)(2,1)S(1)} %get-tuple-element.402) | copy-start | bytes 196612
  77.1 33.1 %copy-start.45 = (f32[512]{0:T(512)}, f32[512]{0:T(512)S(1)}, u32[]{:S(2)}) copy-start(f32[512]{0:T(512)S(1)} %get-tuple-element.413) | copy-start | bytes 6148
  77.9 14.3 %collective-permute-start.1 = (bf16[1024]{0:T(1024)(128)(2,1)S(1)}, bf16[1024]{0:T(1024)(128)(2,1)S(1)}, u32[]{:S(2)}, u32[]{:S(2)}) collective-permute-start(bf16[1024]{0:T(1024)(128)(2,1)S(1)} %get-tuple-element.411), channel_id=1, source_target_pairs={{0,24},{8,32},{16,40},{24,48},{32,56},{40,64},{48,72},{56,80},{64,... | collective-permute-start | bytes 6152 | tf_op jit(solution)/shard_map/ppermute | solution.py:18
  86.3 9.6 %collective-permute-start = (bf16[1024]{0:T(1024)(128)(2,1)S(1)}, bf16[1024]{0:T(1024)(128)(2,1)S(1)}, u32[]{:S(2)}, u32[]{:S(2)}) collective-permute-start(bf16[1024]{0:T(1024)(128)(2,1)S(1)} %get-tuple-element.411), channel_id=1, source_target_pairs={{0,32},{8,40},{16,48},{24,56},{32,64},{40,72},{48,80},{56,88},{64,... | collective-permute-start | bytes 6152 | tf_op jit(solution)/shard_map/ppermute | solution.py:18
  92.1 36.2 %collective-permute-start.10 = (bf16[1024,128]{1,0:T(8,128)(2,1)S(1)}, bf16[1024,128]{1,0:T(8,128)(2,1)}, u32[]{:S(2)}, u32[]{:S(2)}) collective-permute-start(bf16[1024,128]{1,0:T(8,128)(2,1)S(1)} %copy-done.10), channel_id=1, source_target_pairs={{0,32},{8,40},{16,48},{24,56},{32,64},{40,72},{48,80},{56,88},{64,... | collective-permute-start | bytes 786440 | tf_op jit(solution)/shard_map/ppermute | solution.py:18
  95.9 32.4 %collective-permute-start.8 = (bf16[1024,128]{1,0:T(8,128)(2,1)S(1)}, bf16[1024,128]{1,0:T(8,128)(2,1)}, u32[]{:S(2)}, u32[]{:S(2)}) collective-permute-start(bf16[1024,128]{1,0:T(8,128)(2,1)S(1)} %copy-done.10), channel_id=1, source_target_pairs={{0,24},{8,32},{16,40},{24,48},{32,56},{40,64},{48,72},{56,80},{64,... | collective-permute-start | bytes 786440 | tf_op jit(solution)/shard_map/ppermute | solution.py:18
  98.4 29.9 %collective-permute-start.11 = (bf16[1024,128]{1,0:T(8,128)(2,1)}, bf16[1024,128]{1,0:T(8,128)(2,1)}, u32[]{:S(2)}, u32[]{:S(2)}) collective-permute-start(bf16[1024,128]{1,0:T(8,128)(2,1)} %param.30), channel_id=1, source_target_pairs={{0,32},{8,40},{16,48},{24,56},{32,64},{40,72},{48,80},{56,88},{64,... | collective-permute-start | bytes 786440 | tf_op jit(solution)/shard_map/ppermute | solution.py:18
  102.4 25.9 %collective-permute-start.9 = (bf16[1024,128]{1,0:T(8,128)(2,1)}, bf16[1024,128]{1,0:T(8,128)(2,1)}, u32[]{:S(2)}, u32[]{:S(2)}) collective-permute-start(bf16[1024,128]{1,0:T(8,128)(2,1)} %param.30), channel_id=1, source_target_pairs={{0,24},{8,32},{16,40},{24,48},{32,56},{40,64},{48,72},{56,80},{64,... | collective-permute-start | bytes 786440 | tf_op jit(solution)/shard_map/ppermute | solution.py:18
  107.2 20.9 %collective-permute-start.7 = (bf16[1024,128]{1,0:T(8,128)(2,1)}, bf16[1024,128]{1,0:T(8,128)(2,1)}, u32[]{:S(2)}, u32[]{:S(2)}) collective-permute-start(bf16[1024,128]{1,0:T(8,128)(2,1)} %param.30), channel_id=1, source_target_pairs={{0,16},{8,24},{16,32},{24,40},{32,48},{40,56},{48,64},{56,72},{64,... | collective-permute-start | bytes 786440 | tf_op jit(solution)/shard_map/ppermute | solution.py:18
  128.6 43.1 %copy-start.47 = (f32[512]{0:T(512)}, f32[512]{0:T(512)S(1)}, u32[]{:S(2)}) copy-start(f32[512]{0:T(512)S(1)} %negate_divide_fusion.1) | copy-start | bytes 6148
  129.1 42.7 %copy-start.14 = (f32[512]{0:T(512)S(1)}, f32[512]{0:T(512)}, u32[]{:S(2)}) copy-start(f32[512]{0:T(512)} %copy-done.13) | copy-start | bytes 6148
  129.2 42.6 %copy-start.48 = (f32[512]{0:T(512)}, f32[512]{0:T(512)S(1)}, u32[]{:S(2)}) copy-start(f32[512]{0:T(512)S(1)} %negate_divide_fusion) | copy-start | bytes 6148
  201.3 17.7 %all-to-all-start.3 = ((bf16[8,1024,16]{1,2,0:T(8,128)(2,1)}), bf16[8,1024,16]{1,2,0:T(8,128)(2,1)S(1)}, u32[]{:S(2)}, u32[]{:S(2)}) async-start(bf16[8,1024,16]{1,2,0:T(8,128)(2,1)} %bitcast.993), calls=%async_computation.3 | async-start | bytes 524288 | tf_op jit(solution)/shard_map/all_to_all | solution.py:115
  219.9 22.9 %all-to-all-start.1 = ((bf16[32,128,64]{1,2,0:T(8,128)(2,1)}), bf16[32,128,64]{1,2,0:T(8,128)(2,1)S(1)}, u32[]{:S(2)}, u32[]{:S(2)}) async-start(bf16[32,128,64]{1,2,0:T(8,128)(2,1)} %broadcast_in_dim.125), calls=%async_computation.1 | async-start | bytes 1048576 | tf_op jit(solution)/shard_map/all_to_all | solution.py:121
  243.7 15.2 %all-to-all-start = ((bf16[32,1,128,64]{2,3,1,0:T(8,128)(2,1)}), bf16[32,1,128,64]{2,3,1,0:T(8,128)(2,1)S(1)}, u32[]{:S(2)}, u32[]{:S(2)}) async-start(bf16[32,1,128,64]{2,3,1,0:T(8,128)(2,1)} %broadcast_in_dim.124), calls=%async_computation | async-start | bytes 1048576 | tf_op jit(solution)/shard_map/all_to_all | solution.py:121
  259.6 12.9 %all-to-all-start.2 = ((bf16[8,128,64]{1,2,0:T(8,128)(2,1)}), bf16[8,128,64]{1,2,0:T(8,128)(2,1)S(1)}, u32[]{:S(2)}, u32[]{:S(2)}) async-start(bf16[8,128,64]{1,2,0:T(8,128)(2,1)} %broadcast_in_dim.132), calls=%async_computation.2 | async-start | bytes 262144 | tf_op jit(solution)/shard_map/all_to_all | solution.py:121
  (36 other events, 353.5 us)
where the time goes:
time: 276 us; the launch traced here: 273 us
  starting transfers between devices  72.7 us (26%)
  blocking collectives  58.9 us (21%)
  between operations  48.3 us (18%)
  waiting for transfers between devices  36.4 us (13%)
  matrix products  31.8 us (12%)
  other arithmetic  12.6 us (5%)
  local copies, waits for them, and re-layouts  11.9 us (4%)
    all_gather x6, blocking collectives, collected_together(): both, at, found = (lax.all_gather(jnp.concatenate(lines), axis), 0, {})  58.9 us
    ppermute x12, starting transfers between devices, passed_along(): return lax.ppermute(block, axis, route)  46 us
    all_to_all x3, waiting for transfers between devices, sent_to_all(): lax.all_to_all(jnp.broadcast_to(array[None], (size, *array.shape)), axis,...  29.7 us
    all_to_all x3, starting transfers between devices, sent_to_all(): lax.all_to_all(jnp.broadcast_to(array[None], (size, *array.shape)), axis,...  18.4 us
    all_to_all x1, starting transfers between devices, sum_at_owner(): lax.all_to_all(parts, axis, split_axis=0, concat_axis=0, tiled=True)  8.33 us
    all_to_all x1, waiting for transfers between devices, sum_at_owner(): lax.all_to_all(parts, axis, split_axis=0, concat_axis=0, tiled=True)  6.7 us
  transfers between devices with their start and end apart: 16, of which 4 were waited for; matrix products, arithmetic and copies ran while one was open for 13% of the time, Pallas kernels for 0%

commit v1 on v0

v1 whole, which is shorter than its diff:
```python
import functools

import jax
import jax.numpy as jnp
from jax import lax
from jax.experimental import pallas as pl
from jax.experimental.pallas import tpu as pltpu
from jax.sharding import PartitionSpec as P

F32 = jnp.float32
BF16 = jnp.bfloat16
MESH = pl.DeviceIdType.MESH
VMEM = pltpu.VMEM

REACH = 4
SIDE = 4
NEGATIVE = -1e30
LOG2E = 1.4426950408889634
OWN_TILE = 256
FAR_TILE = 512
ADJ_ROWS = 144


def dot(a, b, ca, cb):
    return lax.dot_general(a, b, (((ca,), (cb,)), ((), ())), preferred_element_type=F32)


def remote(src, dst, send_sem, recv_sem, **where):
    return pltpu.make_async_remote_copy(
        src_ref=src,
        dst_ref=dst,
        send_sem=send_sem,
        recv_sem=recv_sem,
        device_id=where,
        device_id_type=MESH,
    )


def signal(sem, **where):
    pl.semaphore_signal(sem, inc=1, device_id=where, device_id_type=MESH)


def window_kernel(
    n_seq,
    n_z,
    k_ref,
    v_ref,
    c_ref,
    wk_ref,
    wv_ref,
    wc_ref,
    code_send,
    code_recv,
    slice_send,
    slice_recv,
    own_send,
    ring_send,
    ring_recv,
    pair_send,
    pair_recv,
):
    s = lax.axis_index("seq")
    z = lax.axis_index("tensor")
    core = lax.rem(s, 2)
    partner = s + 1 - 2 * core
    part = k_ref.shape[0] // n_z

    def later(d):
        return lax.rem(s + d, n_seq)

    def turn(d):
        return lax.rem(z + d + n_z, n_z)

    def rows(p):
        return pl.ds(pl.multiple_of(p * part, part), part)

    barrier = pltpu.get_barrier_semaphore()
    for d in range(1, REACH + 1):
        signal(barrier, seq=later(n_seq - d))
    signal(barrier, seq=partner)
    signal(barrier, tensor=turn(1))
    signal(barrier, tensor=turn(-1))
    pl.semaphore_wait(barrier, REACH + 3)

    pairs = ((k_ref, wk_ref), (v_ref, wv_ref))
    started = []
    for target, (distance, slot) in enumerate(((4 - core, 3 - core), (3 - core, 2 - core))):
        for kv, (own, window) in enumerate(pairs):
            copy = remote(
                own.at[rows(z)],
                window.at[slot, rows(z)],
                slice_send.at[target, kv],
                slice_recv.at[core, kv],
                seq=later(distance),
            )
            copy.start()
            started.append(copy)
    for d in range(1, REACH + 1):
        copy = remote(
            c_ref, wc_ref.at[d - 1], code_send.at[d - 1], code_recv.at[d - 1], seq=later(d)
        )
        copy.start()
        started.append(copy)

    @pl.when(core == 0)
    def _():
        for kv, (own, window) in enumerate(pairs):
            remote(own, window.at[0], own_send.at[kv], pair_recv.at[kv], seq=partner).start()

    slots = (3 - core, 2 - core)

    def pass_to_partner(i, kv, piece):
        window = pairs[kv][1]

        def send(slot):
            remote(
                window.at[slots[i], rows(piece)],
                window.at[slot, rows(piece)],
                pair_send.at[i, kv],
                pair_recv.at[kv],
                seq=partner,
            ).start()

        if i == 1:
            send(3 - 3 * core)
        else:

            @pl.when(core == 1)
            def _():
                send(1)

    def ring_copy(way, step, i, kv):
        window = pairs[kv][1]
        piece = turn(1 - step) if way == 0 else turn(step - 1)
        return remote(
            window.at[slots[i], rows(piece)],
            window.at[slots[i], rows(piece)],
            ring_send.at[way, step - 1, i, kv],
            ring_recv.at[way, step - 1, i, kv],
            tensor=turn(1 if way == 0 else -1),
        )

    last = n_z // 2

    def active(way, step, i):
        return step < last or (step == last and way == i)

    for i in range(2):
        for kv in range(2):
            window = pairs[kv][1]
            here = window.at[slots[i], rows(z)]
            remote(
                here, here, slice_send.at[0, kv], slice_recv.at[i, kv], seq=partner
            ).wait_recv()
            for way in range(2):
                copy = ring_copy(way, 1, i, kv)
                copy.start()
                started.append(copy)
            pass_to_partner(i, kv, z)
    for step in range(1, last + 1):
        for i in range(2):
            for kv in range(2):
                for way in range(2):
                    if not active(way, step, i):
                        continue
                    window = pairs[kv][1]
                    piece = turn(-step) if way == 0 else turn(step)
                    here = window.at[slots[i], rows(piece)]
                    remote(
                        here,
                        here,
                        ring_send.at[way, step - 1, i, kv],
                        ring_recv.at[way, step - 1, i, kv],
                        tensor=turn(1 if way == 0 else -1),
                    ).wait_recv()
                    if active(way, step + 1, i):
                        copy = ring_copy(way, step + 1, i, kv)
                        copy.start()
                        started.append(copy)
                    pass_to_partner(i, kv, piece)

    for copy in started:
        copy.wait_send()
    for d in range(1, REACH + 1):
        remote(
            c_ref, wc_ref.at[d - 1], code_send.at[d - 1], code_recv.at[d - 1], seq=later(d)
        ).wait_recv()
    for kv, (own, window) in enumerate(pairs):
        both = window.at[pl.ds(0, 2)]
        remote(both, both, own_send.at[kv], pair_recv.at[kv], seq=partner).wait_recv()
        whole = window.at[0]
        remote(whole, whole, pair_send.at[1, kv], pair_recv.at[kv], seq=partner).wait_send()

        @pl.when(core == 1)
        def _():
            remote(whole, whole, pair_send.at[0, kv], pair_recv.at[kv], seq=partner).wait_send()

        @pl.when(core == 0)
        def _():
            remote(own, whole, own_send.at[kv], pair_recv.at[kv], seq=partner).wait_send()


def whole(n):
    return [pl.BlockSpec(memory_space=VMEM)] * n


def window_of(keys, values, codes, n_seq, n_z):
    block = (REACH, *keys.shape)
    dma = pltpu.SemaphoreType.DMA
    return pl.pallas_call(
        functools.partial(window_kernel, n_seq, n_z),
        out_shape=(
            jax.ShapeDtypeStruct(block, keys.dtype),
            jax.ShapeDtypeStruct(block, values.dtype),
            jax.ShapeDtypeStruct((REACH, *codes.shape), codes.dtype),
        ),
        in_specs=whole(3),
        out_specs=tuple(whole(3)),
        scratch_shapes=[
            dma((REACH,)),
            dma((REACH,)),
            dma((2, 2)),
            dma((2, 2)),
            dma((2,)),
            dma((2, n_z // 2, 2, 2)),
            dma((2, n_z // 2, 2, 2)),
            dma((2, 2)),
            dma((2,)),
        ],
        compiler_params=pltpu.CompilerParams(collective_id=0, has_side_effects=True),
        name="window",
    )(keys, values, codes)


def features(rows, weights_t):
    logits = dot(weights_t, rows, 1, 1)
    up = jnp.exp(logits - jnp.max(logits, axis=0, keepdims=True))
    down = jnp.exp(jnp.min(logits, axis=0, keepdims=True) - logits)
    up = up / jnp.sum(up, axis=0, keepdims=True)
    down = down / jnp.sum(down, axis=0, keepdims=True)
    return jnp.concatenate([up, down], axis=0)


def features_back(feat, grad):
    half = feat.shape[0] // 2
    p, m, a, b = feat[:half], feat[half:], grad[:half], grad[half:]
    upper = p * (a - jnp.sum(a * p, axis=0, keepdims=True))
    lower = m * (b - jnp.sum(b * m, axis=0, keepdims=True))
    return upper - lower


def transposed(x):
    return x.astype(F32).T.astype(x.dtype)


def lane_copies(row, count):
    return jnp.broadcast_to(row, (count, row.shape[1])).T


def across(column, width):
    return jnp.concatenate([column] * (width // column.shape[1]), axis=1)


def attend_kernel(
    grad_scale,
    q_ref,
    k_ref,
    v_ref,
    c_ref,
    wk_ref,
    wv_ref,
    wc_ref,
    wq_ref,
    wkey_ref,
    student_ref,
    gkf_ref,
    adj_ref,
    gwq_ref,
    kf_ref,
    kcol_ref,
    fcol_ref,
    vt_ref,
    fvt_ref,
    kfb_ref,
    top_ref,
    sum_ref,
    acc_ref,
    num_ref,
    den_ref,
    state_ref,
    ssum_ref,
    qf_ref,
    gqf_ref,
):
    count, width = q_ref.shape
    factor = width**-0.5 * LOG2E
    code = c_ref[...].astype(F32)
    leading = code[:, :1]
    lead = (code == leading).astype(F32)

    wkey_t = transposed(wkey_ref[...])
    kf = features(k_ref[...], wkey_t)
    kf_ref[...] = kf
    kft = kf.astype(BF16)
    kfb_ref[...] = kf.T.astype(BF16)
    qf = features(q_ref[...], transposed(wq_ref[0]))
    qf_ref[...] = qf
    qft = qf.astype(BF16)
    vt_ref[...] = transposed(v_ref[...])
    kcol_ref[...] = lane_copies(code, width)

    def own_mask(start, size, limit):
        same = across(kcol_ref[:limit], size) == code[:, start : start + size]
        key_at = lax.broadcasted_iota(jnp.int32, (limit, size), 0)
        query_at = lax.broadcasted_iota(jnp.int32, (limit, size), 1) + start
        return same & (key_at <= query_at)

    for start in range(0, count, OWN_TILE):
        limit = start + OWN_TILE
        cols = slice(start, limit)
        mask = own_mask(start, OWN_TILE, limit)
        scores = dot(k_ref[:limit], q_ref[cols], 1, 1)
        scores = jnp.where(mask, scores * factor, NEGATIVE)
        top = jnp.max(scores, axis=0, keepdims=True)
        weights = jnp.exp2(scores - top)
        top_ref[:, cols] = top
        sum_ref[:, cols] = jnp.sum(weights, axis=0, keepdims=True)
        acc_ref[:, cols] = dot(vt_ref[:, :limit], weights.astype(BF16), 1, 0)
        products = jnp.where(mask, dot(kfb_ref[:limit], qft[:, cols], 1, 0), 0.0)
        den_ref[:, cols] = jnp.sum(products, axis=0, keepdims=True)
        num_ref[:, cols] = dot(vt_ref[:, :limit], products.astype(BF16), 1, 0)

    state_ref[...] = jnp.zeros_like(state_ref)
    ssum_ref[...] = jnp.zeros_like(ssum_ref)

    def far_block(d, carry):
        far_code = wc_ref[d].astype(F32)
        shared = (far_code == leading).astype(F32)

        @pl.when(jnp.max(shared) > 0.0)
        def _():
            fcol_ref[...] = lane_copies(far_code, width)
            fvt_ref[...] = transposed(wv_ref[d])
            chosen = features(wk_ref[d], wkey_t).astype(BF16).astype(F32) * shared
            state_ref[...] += dot(chosen.astype(BF16), wv_ref[d], 1, 0)
            ssum_ref[...] += jnp.broadcast_to(
                jnp.sum(chosen, axis=1, keepdims=True), ssum_ref.shape
            )
            for first in range(0, count, FAR_TILE):
                cols = slice(first, first + FAR_TILE)
                for at in range(0, count, FAR_TILE):
                    keys = slice(at, at + FAR_TILE)
                    met = (far_code[:, keys] == code[:, first : first + 1]).astype(F32)

                    @pl.when(jnp.max(met) > 0.0)
                    def _(cols=cols, keys=keys):
                        mask = across(fcol_ref[keys], FAR_TILE) == code[:, cols]
                        scores = dot(wk_ref[d, keys], q_ref[cols], 1, 1)
                        scores = jnp.where(mask, scores * factor, NEGATIVE)
                        old = top_ref[:, cols]
                        top = jnp.maximum(old, jnp.max(scores, axis=0, keepdims=True))
                        weights = jnp.exp2(scores - top)
                        shrink = jnp.exp2(old - top)
                        top_ref[:, cols] = top
                        sum_ref[:, cols] = sum_ref[:, cols] * shrink + jnp.sum(
                            weights, axis=0, keepdims=True
                        )
                        acc_ref[:, cols] = acc_ref[:, cols] * shrink + dot(
                            fvt_ref[:, keys], weights.astype(BF16), 1, 0
                        )

        return carry

    lax.fori_loop(0, REACH, far_block, 0)

    state = state_ref[...]
    state_b = state.astype(BF16)
    state_sum = ssum_ref[:, :1]
    teacher = acc_ref[...] / sum_ref[...]
    numerator = num_ref[...] + lead * dot(state.T.astype(BF16), qft, 1, 0)
    denominator = den_ref[...] + lead * jnp.sum(
        qft.astype(F32) * state_sum, axis=0, keepdims=True
    )
    estimate = numerator / denominator
    student_ref[...] = estimate.T.astype(BF16).reshape(student_ref.shape)
    grad_out = grad_scale * (estimate - teacher)
    grad_num = grad_out / denominator
    grad_den = -jnp.sum(grad_out * estimate, axis=0, keepdims=True) / denominator
    gnt = grad_num.astype(BF16)

    extra = ADJ_ROWS - width
    row = lax.broadcasted_iota(jnp.int32, (extra, count), 0)
    tail = jnp.where(row == 0, grad_den * lead, 0.0)
    masked = jnp.concatenate([grad_num * lead, tail], axis=0).astype(BF16)
    adjoint = dot(masked, qft, 1, 1)
    mark = lax.broadcasted_iota(jnp.int32, adjoint.shape, 0)
    adj_ref[...] = jnp.where(mark == width + 1, leading, adjoint).astype(BF16)

    gqf_ref[...] = lead * (dot(state_b, gnt, 1, 0) + state_sum * grad_den)
    for start in range(0, count, OWN_TILE):
        limit = start + OWN_TILE
        cols = slice(start, limit)
        mask = own_mask(start, OWN_TILE, limit)
        grad_prod = dot(v_ref[:limit], gnt[:, cols], 1, 0) + grad_den[:, cols]
        grad_prod = jnp.where(mask, grad_prod, 0.0).astype(BF16)
        gqf_ref[:, cols] += dot(kft[:, :limit], grad_prod, 1, 0)
        part = dot(qft[:, cols], grad_prod, 1, 1)
        if start:
            gkf_ref[:, :start] += part[:, :start]
        gkf_ref[:, cols] = part[:, start:]
    grad_aq = features_back(qf_ref[...], gqf_ref[...]).astype(BF16)
    gwq_ref[...] = dot(grad_aq, q_ref[...], 1, 0)


def attend(queries, keys, values, codes, wk, wv, wc, w_query, w_key, grad_scale):
    count, width = keys.shape
    half = w_key.shape[1]
    feat = 2 * half
    return pl.pallas_call(
        functools.partial(attend_kernel, grad_scale),
        out_shape=(
            jax.ShapeDtypeStruct((count, width), BF16),
            jax.ShapeDtypeStruct((feat, count), F32),
            jax.ShapeDtypeStruct((ADJ_ROWS, feat), BF16),
            jax.ShapeDtypeStruct((half, width), F32),
            jax.ShapeDtypeStruct((feat, count), F32),
        ),
        in_specs=whole(9),
        out_specs=tuple(whole(5)),
        scratch_shapes=[
            VMEM((count, width), F32),
            VMEM((count, width), F32),
            VMEM((width, count), BF16),
            VMEM((width, count), BF16),
            VMEM((count, feat), BF16),
            VMEM((1, count), F32),
            VMEM((1, count), F32),
            VMEM((width, count), F32),
            VMEM((width, count), F32),
            VMEM((1, count), F32),
            VMEM((feat, width), F32),
            VMEM((feat, width), F32),
            VMEM((feat, count), F32),
            VMEM((feat, count), F32),
        ],
        name="attend",
    )(queries, keys, values, codes, wk, wv, wc, w_query, w_key)


def finish_kernel(
    n_seq,
    n_z,
    total,
    adj_ref,
    gkf_ref,
    kf_ref,
    k_ref,
    v_ref,
    c_ref,
    gwq_ref,
    gwq_out,
    gwk_out,
    kfg_out,
    adj_in,
    spread_ref,
    gather_ref,
    core_ref,
    y_ref,
    x_ref,
    z_ref,
    adj_send,
    adj_recv,
    spread_send,
    spread_recv,
    core_send,
    core_recv,
    y_send,
    y_recv,
    x_send,
    x_recv,
    z_send,
    z_recv,
):
    s = lax.axis_index("seq")
    z = lax.axis_index("tensor")
    core = lax.rem(s, 2)
    partner = s + 1 - 2 * core
    y = lax.rem(s // 2, SIDE)
    x = s // (2 * SIDE)
    count, width = k_ref.shape
    half = gwq_ref.shape[0]
    share = kf_ref.shape[0] // n_z

    def along_y(i):
        return lax.rem(y + i, SIDE)

    def along_x(i):
        return lax.rem(x + i, SIDE)

    def along_z(i):
        return lax.rem(z + i, n_z)

    def seq_of(at_x, at_y):
        return (at_x * SIDE + at_y) * 2 + core

    barrier = pltpu.get_barrier_semaphore()
    for d in range(1, REACH + 1):
        signal(barrier, seq=lax.rem(s + d, n_seq))
    signal(barrier, seq=partner)
    for i in range(1, SIDE):
        signal(barrier, seq=seq_of(x, along_y(i)))
        signal(barrier, seq=seq_of(along_x(i), y))
    for i in range(1, n_z):
        signal(barrier, tensor=along_z(i))
    pl.semaphore_wait(barrier, REACH + 1 + 2 * (SIDE - 1) + n_z - 1)

    started = []

    def send(*args, **where):
        copy = remote(*args, **where)
        copy.start()
        started.append(copy)

    for d in range(1, REACH + 1):
        send(
            adj_ref,
            adj_in.at[d - 1],
            adj_send.at[d - 1],
            adj_recv.at[d - 1],
            seq=lax.rem(s + n_seq - d, n_seq),
        )
    code = c_ref[...].astype(F32)
    final = code[:, count - 1 :]
    vt = v_ref[...].astype(F32).T
    one = lax.broadcasted_iota(jnp.int32, (ADJ_ROWS - width, count), 0) == 0
    vt = jnp.concatenate([vt, one.astype(F32)], axis=0).astype(BF16)
    back = (code == final).astype(F32)

    entering = jnp.zeros(adj_ref.shape, F32)
    for d in range(1, REACH + 1):
        here = adj_in.at[d - 1]
        remote(here, here, adj_send.at[d - 1], adj_recv.at[d - 1], seq=partner).wait_recv()
        arrived = adj_in[d - 1].astype(F32)
        entering = entering + jnp.where(arrived[width + 1 : width + 2] == final, arrived, 0.0)
    added = dot(transposed(entering.astype(BF16)), vt, 1, 0)
    grad_kf = gkf_ref[...] + back * added
    spread_ref[...] = (grad_kf * total).astype(BF16)
    for i in range(1, n_z):
        to = along_z(i)
        send(
            spread_ref.at[pl.ds(pl.multiple_of(to * share, share), share)],
            gather_ref.at[z],
            spread_send.at[i - 1],
            spread_recv.at[z],
            tensor=to,
        )
    gather_ref[z] = spread_ref[pl.ds(pl.multiple_of(z * share, share), share)]

    grad_ak = features_back(kf_ref[...], grad_kf).astype(BF16)
    grad_wk = dot(grad_ak, k_ref[...], 1, 0)
    core_ref[core] = jnp.concatenate([gwq_ref[...], grad_wk], axis=0).astype(BF16)

    def wait(ref, at, send_sems, recv_sems):
        here = ref.at[at]
        remote(here, here, send_sems.at[0], recv_sems.at[at], seq=partner).wait_recv()

    def summed(ref):
        result = ref[0].astype(F32)
        for i in range(1, ref.shape[0]):
            result = result + ref[i].astype(F32)
        return result

    send(core_ref.at[core], core_ref.at[core], core_send.at[0], core_recv.at[core], seq=partner)
    wait(core_ref, 1 - core, core_send, core_recv)
    y_ref[y] = summed(core_ref).astype(BF16)
    for i in range(1, SIDE):
        to = seq_of(x, along_y(i))
        send(y_ref.at[y], y_ref.at[y], y_send.at[i - 1], y_recv.at[y], seq=to)
    for i in range(1, SIDE):
        wait(y_ref, along_y(i), y_send, y_recv)
    x_ref[x] = summed(y_ref).astype(BF16)
    for i in range(1, SIDE):
        to = seq_of(along_x(i), y)
        send(x_ref.at[x], x_ref.at[x], x_send.at[i - 1], x_recv.at[x], seq=to)
    for i in range(1, SIDE):
        wait(x_ref, along_x(i), x_send, x_recv)
    over_seq = summed(x_ref)
    z_ref[z] = over_seq[half:].astype(BF16)
    for i in range(1, n_z):
        send(z_ref.at[z], z_ref.at[z], z_send.at[i - 1], z_recv.at[z], tensor=along_z(i))
    gwq_out[...] = over_seq[:half].T.reshape(gwq_out.shape)
    for i in range(1, n_z):
        wait(gather_ref, along_z(i), spread_send, spread_recv)
    kfg_out[...] = summed(gather_ref).T
    for i in range(1, n_z):
        wait(z_ref, along_z(i), z_send, z_recv)
    gwk_out[...] = summed(z_ref).T
    for copy in started:
        copy.wait_send()


def finish(adjoint, grad_kf, key_feat, keys, values, codes, gwq, n_seq, n_z, total):
    count, width = keys.shape
    feat = key_feat.shape[0]
    half = feat // 2
    dma = pltpu.SemaphoreType.DMA
    return pl.pallas_call(
        functools.partial(finish_kernel, n_seq, n_z, total),
        out_shape=(
            jax.ShapeDtypeStruct((1, width, half), F32),
            jax.ShapeDtypeStruct((width, half), F32),
            jax.ShapeDtypeStruct((count, feat // n_z), F32),
        ),
        in_specs=whole(7),
        out_specs=tuple(whole(3)),
        scratch_shapes=[
            VMEM((REACH, ADJ_ROWS, feat), BF16),
            VMEM((feat, count), BF16),
            VMEM((n_z, feat // n_z, count), BF16),
            VMEM((2, feat, width), BF16),
            VMEM((SIDE, feat, width), BF16),
            VMEM((SIDE, feat, width), BF16),
            VMEM((n_z, half, width), BF16),
            dma((REACH,)),
            dma((REACH,)),
            dma((n_z - 1,)),
            dma((n_z,)),
            dma((1,)),
            dma((2,)),
            dma((SIDE - 1,)),
            dma((SIDE,)),
            dma((SIDE - 1,)),
            dma((SIDE,)),
            dma((n_z - 1,)),
            dma((n_z,)),
        ],
        compiler_params=pltpu.CompilerParams(collective_id=1, has_side_effects=True),
        name="finish",
    )(adjoint, grad_kf, key_feat, keys, values, codes, gwq)


def solution(mesh):
    n_seq, n_z = mesh.shape["seq"], mesh.shape["tensor"]

    def shards(queries, keys, values, doc_ids, w_query, w_key):
        count, width = keys.shape
        codes = (doc_ids + 1).reshape(1, count)
        wk, wv, wc = window_of(keys, values, codes, n_seq, n_z)
        student, grad_kf, adjoint, gwq, key_feat = attend(
            queries.reshape(count, width),
            keys,
            values,
            codes,
            wk,
            wv,
            wc,
            w_query,
            w_key,
            2.0 / (count * n_seq),
        )
        grad_wq, grad_wk, key_feature_grads = finish(
            adjoint, grad_kf, key_feat, keys, values, codes, gwq, n_seq, n_z, float(count * n_seq)
        )
        return student.reshape(queries.shape), grad_wq, grad_wk, key_feature_grads

    return jax.shard_map(
        shards,
        mesh=mesh,
        in_specs=(
            P("seq", "tensor", None),
            P("seq", None),
            P("seq", None),
            P("seq"),
            P("tensor", None, None),
            P(),
        ),
        out_specs=(P("seq", "tensor", None), P("tensor", None, None), P(), P("seq", "tensor")),
        check_vma=False,
    )
```

time: 276 us -> 87.9 us (0.32)
  Pallas kernels: 0 us -> 78.5 us
  starting transfers between devices: 72.7 us -> 0 us
  blocking collectives: 58.9 us -> 0 us
  between operations: 48.3 us -> 0.66 us
  waiting for transfers between devices: 36.4 us -> 0 us
  matrix products: 31.8 us -> 0 us
  other arithmetic: 12.6 us -> 1.27 us
  local copies, waits for them, and re-layouts: 11.9 us -> 6.28 us
    pallas_call x0 -> x3, Pallas kernels: none -> 78.5 us  [the longest x1 33.9 us: window_of(): pl.pallas_call(functools.partial(window_kernel, n_seq, n_z), out_shape=(j...]
    all_gather x6 -> x0, blocking collectives: 58.9 us -> none  [collected_together(): both, at, found = (lax.all_gather(jnp.concatenate(lines), axis), 0, {})]
    ppermute x12 -> x0, starting transfers between devices: 46 us -> none  [passed_along(): return lax.ppermute(block, axis, route)]
    all_to_all x4 -> x0, waiting for transfers between devices: 36.4 us -> none  [the longest x3 29.7 us: sent_to_all(): lax.all_to_all(jnp.broadcast_to(array[None], (size, *array.shape)), axis,...]
    dot_general x34 -> x0, matrix products: 31.8 us -> none  [the longest x3 4.67 us: tile_update(): jnp.einsum('qhk,kd->qhd', weights.astype(jnp.bfloat16), value_rows, prefe...]
    all_to_all x4 -> x0, starting transfers between devices: 26.7 us -> none  [the longest x3 18.4 us: sent_to_all(): lax.all_to_all(jnp.broadcast_to(array[None], (size, *array.shape)), axis,...]
    slice x19 -> x0, local copies, waits for them, and re-layouts: 7.42 us -> none  [the longest x4 2.33 us: shards(): piece_codes[-1] == query_codes[0]]
    reduce_sum x14 -> x0, other arithmetic: 5.01 us -> none  [the longest x3 1.57 us: feature_back(): jnp.sum(grad_upper * upper_half, axis=-1, keepdims=True)]
  transfers between devices with their start and end apart: 16 -> 0, of which waited for: 4 -> 0; matrix products, arithmetic and copies ran while one was open for 13% -> 0% of each run, Pallas kernels for 0% -> 0%
where the time goes in v1:
time: 87.9 us; the launch traced here: 86.7 us
  Pallas kernels  78.5 us (89%)
  local copies, waits for them, and re-layouts  6.28 us (7%)
  other arithmetic  1.27 us (1%)
    pallas_call x1, Pallas kernels, window_of(): pl.pallas_call(functools.partial(window_kernel, n_seq, n_z), out_shape=(j...  33.9 us
    pallas_call x1, Pallas kernels, finish(): pl.pallas_call(functools.partial(finish_kernel, n_seq, n_z, total), out_s...  31.6 us
    pallas_call x1, Pallas kernels, attend(): pl.pallas_call(functools.partial(attend_kernel, grad_scale), out_shape=(j...  13 us
    unnamed x9, local copies, waits for them, and re-layouts  6.28 us

profile of v1, /device:TPU:1, one launch (start us, length us, event | category | flops | bytes accessed | tf_op | source)
XLA Modules:
  0.0 86.7 jit_solution(8945958469921384130)
XLA Ops:
  0.6 1.3 %broadcast_add_fusion = s32[1024]{0:T(1024)} fusion(s32[1024]{0:T(1024)} %param.9), kind=kLoop, calls=%fused_computation | loop fusion | flops 1024 | bytes 8192 | tf_op jit(solution)/shard_map/add | solution.py:647
  1.9 0.0 copy-start.1
  1.9 1.4 %copy.10.wq_ref = bf16[1,128,64]{2,1,0:T(8,128)(2,1)} copy(bf16[1,128,64]{1,2,0:T(8,128)(2,1)} %param.10) | data formatting | bytes 32768 | tf_op args[4]
  3.4 0.0 copy-done.1
  3.4 0.7 copy.11.wkey_ref
  4.1 33.9 %window.1 = (bf16[4,1024,128]{2,1,0:T(8,128)(2,1)}, bf16[4,1024,128]{2,1,0:T(8,128)(2,1)}, s32[4,1,1024]{2,1,0:T(1,128)}) custom-call(bf16[1024,128]{1,0:T(8,128)(2,1)} %k_ref.5, bf16[1024,128]{1,0:T(8,128)(2,1)} %v_ref.5, s32[1,1024]{1,0:T(1,128)} %bitcast.4), custom_call_target="tpu_custom_call" | custom-call | tf_op jit(solution)/shard_map/window/pallas_call | solution.py:210
  38.0 13.0 %attend.1 = (bf16[1024,128]{1,0:T(8,128)(2,1)}, f32[128,1024]{1,0:T(8,128)}, bf16[144,128]{1,0:T(8,128)(2,1)}, f32[64,128]{1,0:T(8,128)}, f32[128,1024]{1,0:T(8,128)}) custom-call(bf16[1024,128]{1,0:T(8,128)(2,1)} %bitcast.3, bf16[1024,128]{1,0:T(8,128)(2,1)} %k_ref.5, bf16[1024,128]{1,0:T(8,128)(2,1)} %v_ref.5, s32[1,1024]{1,0:T(1,128)} %bitcast.5, ...), custom_call_target="tpu_custom_call" | custom-call | tf_op jit(solution)/shard_map/attend/pallas_call | solution.py:419
  51.0 31.6 %finish.1 = (f32[1,128,64]{2,1,0:T(8,128)}, f32[128,64]{1,0:T(8,128)}, f32[1024,16]{1,0:T(8,128)}) custom-call(bf16[144,128]{1,0:T(8,128)(2,1)} %get-tuple-element.19.adj_ref, f32[128,1024]{1,0:T(8,128)} %get-tuple-element.20.gkf_ref, f32[128,1024]{1,0:T(8,128)} %get-tuple-element.21.kf_ref, bf16[1024,128]{1,0:T(8,128)(2,1)} %k_ref.5, ...), custom_call_target="tpu_custom_call" | custom-call | tf_op jit(solution)/shard_map/finish/pallas_call | solution.py:607
  82.6 0.0 copy-start
  82.6 1.6 %copy.12 = f32[1,128,64]{1,2,0:T(8,128)} copy(f32[1,128,64]{2,1,0:T(8,128)} %get-tuple-element.27) | data formatting | bytes 65536
  84.2 0.0 copy-done
  84.2 0.7 copy.13
  84.9 1.8 %copy.14 = f32[1024,16]{0,1:T(8,128)} copy(f32[1024,16]{1,0:T(8,128)} %get-tuple-element.29) | data formatting | bytes 131072
Async XLA Ops:
  1.9 1.5 %copy-start.1 = (bf16[128,64]{0,1:T(8,128)(2,1)S(1)}, bf16[128,64]{0,1:T(8,128)(2,1)}, u32[]{:S(2)}) copy-start(bf16[128,64]{0,1:T(8,128)(2,1)} %param.11) | copy-start | bytes 49156
  82.6 1.6 %copy-start = (f32[128,64]{1,0:T(8,128)S(1)}, f32[128,64]{1,0:T(8,128)}, u32[]{:S(2)}) copy-start(f32[128,64]{1,0:T(8,128)} %get-tuple-element.28) | copy-start | bytes 98308

commit v2 on v1

v2 whole, which is shorter than its diff:
```python
import functools

import jax
import jax.numpy as jnp
from jax import lax
from jax.experimental import pallas as pl
from jax.experimental.pallas import tpu as pltpu
from jax.sharding import PartitionSpec as P

F32 = jnp.float32
BF16 = jnp.bfloat16
MESH = pl.DeviceIdType.MESH
VMEM = pltpu.VMEM

REACH = 4
SIDE = 4
NEGATIVE = -1e30
LOG2E = 1.4426950408889634
TILE = 256
ADJ_ROWS = 144


def dot(a, b, ca, cb):
    return lax.dot_general(a, b, (((ca,), (cb,)), ((), ())), preferred_element_type=F32)


def remote(src, dst, send_sem, recv_sem, **where):
    return pltpu.make_async_remote_copy(
        src_ref=src,
        dst_ref=dst,
        send_sem=send_sem,
        recv_sem=recv_sem,
        device_id=where,
        device_id_type=MESH,
    )


def signal(sem, **where):
    pl.semaphore_signal(sem, inc=1, device_id=where, device_id_type=MESH)


def features(rows, weights_t):
    logits = dot(weights_t, rows, 1, 1)
    up = jnp.exp(logits - jnp.max(logits, axis=0, keepdims=True))
    down = jnp.exp(jnp.min(logits, axis=0, keepdims=True) - logits)
    up = up / jnp.sum(up, axis=0, keepdims=True)
    down = down / jnp.sum(down, axis=0, keepdims=True)
    return jnp.concatenate([up, down], axis=0)


def features_back(feat, grad):
    half = feat.shape[0] // 2
    p, m, a, b = feat[:half], feat[half:], grad[:half], grad[half:]
    upper = p * (a - jnp.sum(a * p, axis=0, keepdims=True))
    lower = m * (b - jnp.sum(b * m, axis=0, keepdims=True))
    return upper - lower


def transposed(x):
    return x.astype(F32).T.astype(x.dtype)


def lane_copies(row, count):
    return jnp.broadcast_to(row, (count, row.shape[1])).T


def across(column, width):
    return jnp.concatenate([column] * (width // column.shape[1]), axis=1)


def fused_kernel(
    n_seq,
    n_z,
    q_ref,
    k_ref,
    v_ref,
    c_ref,
    wq_ref,
    wkey_ref,
    student_ref,
    gwq_out,
    gwk_out,
    kfg_out,
    wk_ref,
    wv_ref,
    wc_ref,
    kcol_ref,
    fcol_ref,
    vt_ref,
    kfb_ref,
    kf_ref,
    qf_ref,
    top_ref,
    sum_ref,
    den_ref,
    acc_ref,
    num_ref,
    state_ref,
    ssum_ref,
    gqf_ref,
    gkf_ref,
    adj_ref,
    adj_in,
    spread_ref,
    gather_ref,
    core_ref,
    y_ref,
    x_ref,
    z_ref,
    code_send,
    code_recv,
    slice_send,
    slice_recv,
    own_send,
    own_recv,
    ring_send,
    ring_recv,
    pair_send,
    pair_recv,
    adj_send,
    adj_recv,
    spread_send,
    spread_recv,
    core_send,
    core_recv,
    y_send,
    y_recv,
    x_send,
    x_recv,
    z_send,
    z_recv,
):
    count, width = k_ref.shape
    half = wkey_ref.shape[0]
    total = float(count * n_seq)
    grad_scale = 2.0 / total
    factor = width**-0.5 * LOG2E
    s = lax.axis_index("seq")
    z = lax.axis_index("tensor")
    core = lax.rem(s, 2)
    partner = s + 1 - 2 * core
    y = lax.rem(s // 2, SIDE)
    x = s // (2 * SIDE)
    part = count // n_z
    share = 2 * half // n_z

    def later(d):
        return lax.rem(s + d, n_seq)

    def turn(d):
        return lax.rem(z + d + n_z, n_z)

    def along_y(i):
        return lax.rem(y + i, SIDE)

    def along_x(i):
        return lax.rem(x + i, SIDE)

    def seq_of(at_x, at_y):
        return (at_x * SIDE + at_y) * 2 + core

    def rows(p):
        return pl.ds(pl.multiple_of(p * part, part), part)

    barrier = pltpu.get_barrier_semaphore()
    for d in range(1, REACH + 1):
        signal(barrier, seq=later(n_seq - d))
        signal(barrier, seq=later(d))
    signal(barrier, seq=partner)
    for i in range(1, SIDE):
        signal(barrier, seq=seq_of(x, along_y(i)))
        signal(barrier, seq=seq_of(along_x(i), y))
    for i in range(1, n_z):
        signal(barrier, tensor=turn(i))
    pl.semaphore_wait(barrier, 2 * REACH + 1 + 2 * (SIDE - 1) + n_z - 1)

    started = []

    def send(*args, **where):
        copy = remote(*args, **where)
        copy.start()
        started.append(copy)

    def arrive(here, send_sem, recv_sem):
        remote(here, here, send_sem, recv_sem, seq=partner).wait_recv()

    pairs = ((k_ref, wk_ref), (v_ref, wv_ref))
    for target, (distance, slot) in enumerate(((4 - core, 3 - core), (3 - core, 2 - core))):
        for kv, (own, window) in enumerate(pairs):
            send(
                own.at[rows(z)],
                window.at[slot, rows(z)],
                slice_send.at[target, kv],
                slice_recv.at[core, kv],
                seq=later(distance),
            )
    for d in range(1, REACH + 1):
        send(c_ref, wc_ref.at[d - 1], code_send.at[d - 1], code_recv.at[d - 1], seq=later(d))

    @pl.when(core == 0)
    def _():
        for kv, (own, window) in enumerate(pairs):
            remote(own, window.at[0], own_send.at[kv], own_recv.at[kv], seq=partner).start()

    slots = (3 - core, 2 - core)

    def pass_to_partner(i, kv, piece, order):
        window = pairs[kv][1]

        def go(slot):
            remote(
                window.at[slots[i], rows(piece)],
                window.at[slot, rows(piece)],
                pair_send.at[i, kv],
                pair_recv.at[i, kv, order],
                seq=partner,
            ).start()

        if i == 1:
            go(3 - 3 * core)
        else:

            @pl.when(core == 1)
            def _():
                go(1)

    def from_partner(order, piece):
        for kv in range(2):
            here = pairs[kv][1].at[0, rows(piece)]
            arrive(here, pair_send.at[1, kv], pair_recv.at[1, kv, order])

            @pl.when(core == 0)
            def _():
                arrive(here, pair_send.at[0, kv], pair_recv.at[0, kv, order])

    last = n_z // 2

    def active(way, step, i):
        return step < last or (step == last and way == i)

    def ring_copy(way, step, i, kv):
        here = pairs[kv][1].at[slots[i], rows(turn(1 - step) if way == 0 else turn(step - 1))]
        send(
            here,
            here,
            ring_send.at[way, step - 1, i, kv],
            ring_recv.at[way, step - 1, i, kv],
            tensor=turn(1 if way == 0 else -1),
        )

    def ring_step(step):
        for i in range(2):
            for kv in range(2):
                for way in range(2):
                    if not active(way, step, i):
                        continue
                    piece = turn(-step) if way == 0 else turn(step)
                    here = pairs[kv][1].at[slots[i], rows(piece)]
                    arrive(here, ring_send.at[way, step - 1, i, kv], ring_recv.at[way, step - 1, i, kv])
                    if active(way, step + 1, i):
                        ring_copy(way, step + 1, i, kv)
                    pass_to_partner(i, kv, piece, 2 * step - 1 if step == last else 2 * step - 1 + way)

    code = c_ref[...].astype(F32)
    leading = code[:, :1]
    lead = (code == leading).astype(F32)
    wkey_t = wkey_ref[...]
    kf = features(k_ref[...], wkey_t)
    kf_ref[...] = kf
    kft = kf.astype(BF16)
    kfb_ref[...] = kf.T.astype(BF16)
    qf = features(q_ref[...], wq_ref[...])
    qf_ref[...] = qf
    qft = qf.astype(BF16)
    vt_ref[:width] = transposed(v_ref[...])
    one = lax.broadcasted_iota(jnp.int32, (ADJ_ROWS - width, count), 0) == 0
    vt_ref[width:] = one.astype(F32).astype(BF16)
    kcol_ref[...] = lane_copies(code, width)

    def own_mask(start, limit):
        same = across(kcol_ref[:limit], TILE) == code[:, start:limit]
        key_at = lax.broadcasted_iota(jnp.int32, (limit, TILE), 0)
        query_at = lax.broadcasted_iota(jnp.int32, (limit, TILE), 1) + start
        return same & (key_at <= query_at)

    def own_tile(start):
        limit = start + TILE
        cols = slice(start, limit)
        mask = own_mask(start, limit)
        scores = dot(k_ref[:limit], q_ref[cols], 1, 1)
        scores = jnp.where(mask, scores * factor, NEGATIVE)
        top = jnp.max(scores, axis=0, keepdims=True)
        weights = jnp.exp2(scores - top)
        top_ref[:, cols] = top
        sum_ref[:, cols] = jnp.sum(weights, axis=0, keepdims=True)
        acc_ref[:, cols] = dot(vt_ref[:width, :limit], weights.astype(BF16), 1, 0)
        products = jnp.where(mask, dot(kfb_ref[:limit], qft[:, cols], 1, 0), 0.0)
        den_ref[:, cols] = jnp.sum(products, axis=0, keepdims=True)
        num_ref[:, cols] = dot(vt_ref[:width, :limit], products.astype(BF16), 1, 0)

    def far_pieces(pieces):
        places = [(d, rows(p), p) for d in range(REACH) for p in pieces]
        keys = jnp.concatenate([wk_ref[d, r] for d, r, _ in places], axis=0)
        vals = jnp.concatenate([wv_ref[d, r] for d, r, _ in places], axis=0)
        column = jnp.concatenate([fcol_ref[d, r] for d, r, _ in places], axis=0)
        shared = jnp.concatenate([wc_ref[d, :, rows(p)] for d, _, p in places], axis=1)
        shared = (shared.astype(F32) == leading).astype(F32)
        chosen = features(keys, wkey_t).astype(BF16).astype(F32) * shared
        state_ref[...] += dot(chosen.astype(BF16), vals, 1, 0)
        ssum_ref[...] += jnp.broadcast_to(jnp.sum(chosen, axis=1, keepdims=True), ssum_ref.shape)
        vals_t = transposed(vals)
        for start in range(0, count, TILE):
            cols = slice(start, start + TILE)
            mask = across(column, TILE) == code[:, cols]
            scores = dot(keys, q_ref[cols], 1, 1)
            scores = jnp.where(mask, scores * factor, NEGATIVE)
            old = top_ref[:, cols]
            top = jnp.maximum(old, jnp.max(scores, axis=0, keepdims=True))
            weights = jnp.exp2(scores - top)
            shrink = jnp.exp2(old - top)
            top_ref[:, cols] = top
            sum_ref[:, cols] = sum_ref[:, cols] * shrink + jnp.sum(weights, axis=0, keepdims=True)
            acc_ref[:, cols] = acc_ref[:, cols] * shrink + dot(vals_t, weights.astype(BF16), 1, 0)

    for start in range(0, count // 2, TILE):
        own_tile(start)
    for d in range(REACH):
        arrive(wc_ref.at[d], code_send.at[d], code_recv.at[d])
        fcol_ref[d] = lane_copies(wc_ref[d].astype(F32), width)
    state_ref[...] = jnp.zeros_like(state_ref)
    ssum_ref[...] = jnp.zeros_like(ssum_ref)
    for i in range(2):
        for kv in range(2):
            here = pairs[kv][1].at[slots[i], rows(z)]
            arrive(here, slice_send.at[0, kv], slice_recv.at[i, kv])
            for way in range(2):
                ring_copy(way, 1, i, kv)
            pass_to_partner(i, kv, z, 0)
    for start in range(count // 2, count, TILE):
        own_tile(start)

    @pl.when(core == 1)
    def _():
        for kv in range(2):
            arrive(pairs[kv][1].at[0], own_send.at[kv], own_recv.at[kv])

    ring_step(1)
    from_partner(0, z)
    far_pieces((z,))
    for step in range(1, last - 1):
        ring_step(step + 1)
        for way in range(2):
            from_partner(2 * step - 1 + way, turn(-step) if way == 0 else turn(step))
        far_pieces((turn(-step), turn(step)))
    step = last - 1
    for way in range(2):
        from_partner(2 * step - 1 + way, turn(-step) if way == 0 else turn(step))
    far_pieces((turn(-step), turn(step)))
    ring_step(last)
    from_partner(2 * last - 1, turn(last))
    far_pieces((turn(last),))

    state = state_ref[...]
    state_sum = ssum_ref[:, :1]
    teacher = acc_ref[...] / sum_ref[...]
    numerator = num_ref[...] + lead * dot(state.T.astype(BF16), qft, 1, 0)
    denominator = den_ref[...] + lead * jnp.sum(
        qft.astype(F32) * state_sum, axis=0, keepdims=True
    )
    estimate = numerator / denominator
    grad_out = grad_scale * (estimate - teacher)
    grad_num = grad_out / denominator
    grad_den = -jnp.sum(grad_out * estimate, axis=0, keepdims=True) / denominator
    gnt = grad_num.astype(BF16)

    row = lax.broadcasted_iota(jnp.int32, (ADJ_ROWS - width, count), 0)
    tail = jnp.where(row == 0, grad_den * lead, 0.0)
    masked = jnp.concatenate([grad_num * lead, tail], axis=0).astype(BF16)
    adjoint = dot(masked, qft, 1, 1)
    mark = lax.broadcasted_iota(jnp.int32, adjoint.shape, 0)
    adj_ref[...] = jnp.where(mark == width + 1, leading, adjoint).astype(BF16)
    for d in range(1, REACH + 1):
        send(
            adj_ref,
            adj_in.at[d - 1],
            adj_send.at[d - 1],
            adj_recv.at[d - 1],
            seq=later(n_seq - d),
        )

    gqf_ref[...] = lead * (dot(state.astype(BF16), gnt, 1, 0) + state_sum * grad_den)
    for start in range(0, count, TILE):
        limit = start + TILE
        cols = slice(start, limit)
        grad_prod = dot(v_ref[:limit], gnt[:, cols], 1, 0) + grad_den[:, cols]
        grad_prod = jnp.where(own_mask(start, limit), grad_prod, 0.0).astype(BF16)
        gqf_ref[:, cols] += dot(kft[:, :limit], grad_prod, 1, 0)
        piece = dot(qft[:, cols], grad_prod, 1, 1)
        if start:
            gkf_ref[:, :start] += piece[:, :start]
        gkf_ref[:, cols] = piece[:, start:]

    def wait(ref, which, at, send_sems, recv_sems):
        here = ref.at[which, at]
        arrive(here, send_sems.at[which, 0], recv_sems.at[which, at])

    def summed(ref, which):
        result = ref[which, 0].astype(F32)
        for i in range(1, ref.shape[1]):
            result = result + ref[which, i].astype(F32)
        return result

    def over_core(which, value):
        core_ref[which, core] = value.astype(BF16)
        here = core_ref.at[which, core]
        send(here, here, core_send.at[which, 0], core_recv.at[which, core], seq=partner)

    def over_y(which):
        wait(core_ref, which, 1 - core, core_send, core_recv)
        y_ref[which, y] = summed(core_ref, which).astype(BF16)
        here = y_ref.at[which, y]
        for i in range(1, SIDE):
            to = seq_of(x, along_y(i))
            send(here, here, y_send.at[which, i - 1], y_recv.at[which, y], seq=to)

    def over_x(which):
        for i in range(1, SIDE):
            wait(y_ref, which, along_y(i), y_send, y_recv)
        x_ref[which, x] = summed(y_ref, which).astype(BF16)
        here = x_ref.at[which, x]
        for i in range(1, SIDE):
            to = seq_of(along_x(i), y)
            send(here, here, x_send.at[which, i - 1], x_recv.at[which, x], seq=to)

    def over_seq(which):
        for i in range(1, SIDE):
            wait(x_ref, which, along_x(i), x_send, x_recv)
        return summed(x_ref, which)

    grad_aq = features_back(qf_ref[...], gqf_ref[...]).astype(BF16)
    over_core(0, dot(grad_aq, q_ref[...], 1, 0))
    student_ref[...] = estimate.T.astype(BF16)
    over_y(0)

    final = code[:, count - 1 :]
    back = (code == final).astype(F32)
    entering = jnp.zeros(adj_ref.shape, F32)
    for d in range(REACH):
        arrive(adj_in.at[d], adj_send.at[d], adj_recv.at[d])
        arrived = adj_in[d].astype(F32)
        entering = entering + jnp.where(arrived[width + 1 : width + 2] == final, arrived, 0.0)
    added = dot(entering.T.astype(BF16), vt_ref[...], 1, 0)
    grad_kf = gkf_ref[...] + back * added
    spread_ref[...] = (grad_kf * total).astype(BF16)
    for i in range(1, n_z):
        to = turn(i)
        send(
            spread_ref.at[pl.ds(pl.multiple_of(to * share, share), share)],
            gather_ref.at[0, z],
            spread_send.at[0, i - 1],
            spread_recv.at[0, z],
            tensor=to,
        )
    gather_ref[0, z] = spread_ref[pl.ds(pl.multiple_of(z * share, share), share)]

    grad_ak = features_back(kf_ref[...], grad_kf).astype(BF16)
    over_core(1, dot(grad_ak, k_ref[...], 1, 0))
    over_x(0)
    over_y(1)
    gwq_out[...] = over_seq(0)
    over_x(1)
    z_ref[0, z] = over_seq(1).astype(BF16)
    here = z_ref.at[0, z]
    for i in range(1, n_z):
        send(here, here, z_send.at[0, i - 1], z_recv.at[0, z], tensor=turn(i))
    for i in range(1, n_z):
        wait(gather_ref, 0, turn(i), spread_send, spread_recv)
    kfg_out[...] = summed(gather_ref, 0)
    for i in range(1, n_z):
        wait(z_ref, 0, turn(i), z_send, z_recv)
    gwk_out[...] = summed(z_ref, 0)

    for copy in started:
        copy.wait_send()
    for kv, (own, window) in enumerate(pairs):
        block = window.at[0]
        remote(block, block, pair_send.at[1, kv], own_recv.at[kv], seq=partner).wait_send()

        @pl.when(core == 1)
        def _():
            remote(block, block, pair_send.at[0, kv], own_recv.at[kv], seq=partner).wait_send()

        @pl.when(core == 0)
        def _():
            remote(own, block, own_send.at[kv], own_recv.at[kv], seq=partner).wait_send()


def fused(queries, keys, values, codes, wq_t, wkey_t, n_seq, n_z):
    count, width = keys.shape
    half = wkey_t.shape[0]
    feat = 2 * half
    dma = pltpu.SemaphoreType.DMA
    return pl.pallas_call(
        functools.partial(fused_kernel, n_seq, n_z),
        out_shape=(
            jax.ShapeDtypeStruct((count, width), BF16),
            jax.ShapeDtypeStruct((half, width), F32),
            jax.ShapeDtypeStruct((half, width), F32),
            jax.ShapeDtypeStruct((feat // n_z, count), F32),
        ),
        in_specs=[pl.BlockSpec(memory_space=VMEM)] * 6,
        out_specs=(pl.BlockSpec(memory_space=VMEM),) * 4,
        scratch_shapes=[
            VMEM((REACH, count, width), BF16),
            VMEM((REACH, count, width), BF16),
            VMEM((REACH, 1, count), jnp.int32),
            VMEM((count, width), F32),
            VMEM((REACH, count, width), F32),
            VMEM((ADJ_ROWS, count), BF16),
            VMEM((count, feat), BF16),
            VMEM((feat, count), F32),
            VMEM((feat, count), F32),
            VMEM((1, count), F32),
            VMEM((1, count), F32),
            VMEM((1, count), F32),
            VMEM((width, count), F32),
            VMEM((width, count), F32),
            VMEM((feat, width), F32),
            VMEM((feat, width), F32),
            VMEM((feat, count), F32),
            VMEM((feat, count), F32),
            VMEM((ADJ_ROWS, feat), BF16),
            VMEM((REACH, ADJ_ROWS, feat), BF16),
            VMEM((feat, count), BF16),
            VMEM((1, n_z, feat // n_z, count), BF16),
            VMEM((2, 2, half, width), BF16),
            VMEM((2, SIDE, half, width), BF16),
            VMEM((2, SIDE, half, width), BF16),
            VMEM((1, n_z, half, width), BF16),
            dma((REACH,)),
            dma((REACH,)),
            dma((2, 2)),
            dma((2, 2)),
            dma((2,)),
            dma((2,)),
            dma((2, n_z // 2, 2, 2)),
            dma((2, n_z // 2, 2, 2)),
            dma((2, 2)),
            dma((2, 2, n_z)),
            dma((REACH,)),
            dma((REACH,)),
            dma((1, n_z - 1)),
            dma((1, n_z)),
            dma((2, 1)),
            dma((2, 2)),
            dma((2, SIDE - 1)),
            dma((2, SIDE)),
            dma((2, SIDE - 1)),
            dma((2, SIDE)),
            dma((1, n_z - 1)),
            dma((1, n_z)),
        ],
        compiler_params=pltpu.CompilerParams(collective_id=0, has_side_effects=True),
        name="fused",
    )(queries, keys, values, codes, wq_t, wkey_t)


def solution(mesh):
    n_seq, n_z = mesh.shape["seq"], mesh.shape["tensor"]

    def shards(queries, keys, values, doc_ids, w_query, w_key):
        count, width = keys.shape
        student, gwq, gwk, kfg = fused(
            queries.reshape(count, width),
            keys,
            values,
            doc_ids.reshape(1, count),
            w_query[0].T,
            w_key.T,
            n_seq,
            n_z,
        )
        return student.reshape(queries.shape), gwq.T[None], gwk.T, kfg.T

    return jax.shard_map(
        shards,
        mesh=mesh,
        in_specs=(
            P("seq", "tensor", None),
            P("seq", None),
            P("seq", None),
            P("seq"),
            P("tensor", None, None),
            P(),
        ),
        out_specs=(P("seq", "tensor", None), P("tensor", None, None), P(), P("seq", "tensor")),
        check_vma=False,
    )
```

time: 87.9 us -> 66.6 us (0.76)
  Pallas kernels: 78.5 us -> 62 us
  local copies, waits for them, and re-layouts: 6.28 us -> 3.55 us
  other arithmetic: 1.27 us -> 0 us
    pallas_call x3 -> x1, Pallas kernels: 78.5 us -> 62 us  [fused(): pl.pallas_call(functools.partial(fused_kernel, n_seq, n_z), out_shape=(ja...]
    unnamed x9 -> x10, local copies, waits for them, and re-layouts: 6.28 us -> 3.55 us
    add x1 -> x0, other arithmetic: 1.27 us -> none  [shards(): codes = (doc_ids + 1).reshape(1, count)]
where the time goes in v2:
time: 66.6 us; the launch traced here: 66.2 us
  Pallas kernels  62 us (93%)
  local copies, waits for them, and re-layouts  3.55 us (5%)
    pallas_call x1, Pallas kernels, fused(): pl.pallas_call(functools.partial(fused_kernel, n_seq, n_z), out_shape=(ja...  62 us
    unnamed x10, local copies, waits for them, and re-layouts  3.55 us

profile of v2, /device:TPU:1, one launch (start us, length us, event | category | flops | bytes accessed | tf_op | source)
XLA Modules:
  0.0 66.2 jit_solution(8679920965520010032)
XLA Ops:
  0.6 62.0 %fused.1 = (bf16[1024,128]{1,0:T(8,128)(2,1)}, f32[64,128]{1,0:T(8,128)}, f32[64,128]{1,0:T(8,128)}, f32[16,1024]{1,0:T(8,128)}) custom-call(bf16[1024,128]{1,0:T(8,128)(2,1)} %bitcast.12, bf16[1024,128]{1,0:T(8,128)(2,1)} %k_ref.1, bf16[1024,128]{1,0:T(8,128)(2,1)} %v_ref.1, s32[1,1024]{1,0:T(1,128)} %bitcast.19, bf16[64,128]{1,0:T(8,128)(2,1)} %bitcast.17, ...), custom_call_target="tpu_custom_call" | custom-call | tf_op jit(solution)/shard_map/fused/pallas_call | solution.py:503
  62.6 0.0 copy-start.2
  62.6 0.0 copy-start.1
  62.6 1.7 %copy.14 = bf16[1024,1,128]{2,0,1:T(8,128)(2,1)} copy(bf16[1024,1,128]{2,0,1:T(8,128)(2,1)} %bitcast.13) | data formatting | bytes 524288
  64.3 0.0 copy-done.2
  64.3 0.0 copy-start
  64.3 0.6 copy.15
  64.9 0.0 copy-done.1
  64.9 0.6 copy.16
  65.6 0.0 copy-done
  65.6 0.6 copy.17
Async XLA Ops:
  62.6 1.7 %copy-start.2 = (f32[64,128]{1,0:T(8,128)S(1)}, f32[64,128]{1,0:T(8,128)}, u32[]{:S(2)}) copy-start(f32[64,128]{1,0:T(8,128)} %get-tuple-element.9) | copy-start | bytes 98308
  62.6 2.3 %copy-start.1 = (f32[64,128]{1,0:T(8,128)S(1)}, f32[64,128]{1,0:T(8,128)}, u32[]{:S(2)}) copy-start(f32[64,128]{1,0:T(8,128)} %get-tuple-element.10) | copy-start | bytes 98308
  64.3 1.2 %copy-start = (f32[16,1024]{1,0:T(8,128)S(1)}, f32[16,1024]{1,0:T(8,128)}, u32[]{:S(2)}) copy-start(f32[16,1024]{1,0:T(8,128)} %get-tuple-element.11) | copy-start | bytes 196612

commit v3 on v2

--- a/solution.py
+++ b/solution.py
@@ -71,6 +71,16 @@
 def fused_kernel(
     n_seq,
     n_z,
+    q_hbm,
+    k_hbm,
+    v_hbm,
+    c_hbm,
+    wq_hbm,
+    wkey_hbm,
+    student_hbm,
+    gwq_out,
+    gwk_out,
+    kfg_out,
     q_ref,
     k_ref,
     v_ref,
@@ -78,20 +88,16 @@
     wq_ref,
     wkey_ref,
     student_ref,
-    gwq_out,
-    gwk_out,
-    kfg_out,
     wk_ref,
     wv_ref,
     wc_ref,
     kcol_ref,
-    fcol_ref,
+    fkf_ref,
     vt_ref,
     kfb_ref,
     kf_ref,
     qf_ref,
     top_ref,
-    sum_ref,
     den_ref,
     acc_ref,
     num_ref,
@@ -107,10 +113,13 @@
     y_ref,
     x_ref,
     z_ref,
+    load_sem,
+    store_sem,
     code_send,
     code_recv,
     slice_send,
     slice_recv,
+    pass_send,
     own_send,
     own_recv,
     ring_send,
@@ -131,7 +140,7 @@
     z_recv,
 ):
     count, width = k_ref.shape
-    half = wkey_ref.shape[0]
+    half = wkey_hbm.shape[0]
     total = float(count * n_seq)
     grad_scale = 2.0 / total
     factor = width**-0.5 * LOG2E
@@ -162,6 +171,22 @@
     def rows(p):
         return pl.ds(pl.multiple_of(p * part, part), part)
 
+    loads = [
+        pltpu.make_async_copy(far, near, load_sem.at[i])
+        for i, (far, near) in enumerate(
+            (
+                (k_hbm, k_ref),
+                (v_hbm, v_ref),
+                (c_hbm, c_ref),
+                (q_hbm, q_ref),
+                (wq_hbm, wq_ref),
+                (wkey_hbm, wkey_ref),
+            )
+        )
+    ]
+    for load in loads:
+        load.start()
+
     barrier = pltpu.get_barrier_semaphore()
     for d in range(1, REACH + 1):
         signal(barrier, seq=later(n_seq - d))
@@ -172,6 +197,8 @@
         signal(barrier, seq=seq_of(along_x(i), y))
     for i in range(1, n_z):
         signal(barrier, tensor=turn(i))
+    for load in loads:
+        load.wait()
     pl.semaphore_wait(barrier, 2 * REACH + 1 + 2 * (SIDE - 1) + n_z - 1)
 
     started = []
@@ -185,15 +212,36 @@
         remote(here, here, send_sem, recv_sem, seq=partner).wait_recv()
 
     pairs = ((k_ref, wk_ref), (v_ref, wv_ref))
-    for target, (distance, slot) in enumerate(((4 - core, 3 - core), (3 - core, 2 - core))):
+    slots = (3 - core, 2 - core)
+    last = n_z // 2
+    direct = (z, turn(last))
+
+    def send_slice(j):
         for kv, (own, window) in enumerate(pairs):
             send(
-                own.at[rows(z)],
-                window.at[slot, rows(z)],
-                slice_send.at[target, kv],
-                slice_recv.at[core, kv],
-                seq=later(distance),
+                own.at[rows(direct[j])],
+                window.at[2 - core, rows(direct[j])],
+                slice_send.at[j, kv],
+                slice_recv.at[j, core, kv],
+                seq=later(3 - core),
             )
+
+    def take_slice(j, i, kv):
+        window = pairs[kv][1]
+        here = window.at[slots[i], rows(direct[j])]
+        arrive(here, slice_send.at[j, kv], slice_recv.at[j, i, kv])
+
+        @pl.when(core == 1)
+        def _():
+            remote(
+                here,
+                window.at[3 - i, rows(direct[j])],
+                pass_send.at[j, i, kv],
+                slice_recv.at[j, i, kv],
+                seq=later(1),
+            ).start()
+
+    send_slice(0)
     for d in range(1, REACH + 1):
         send(c_ref, wc_ref.at[d - 1], code_send.at[d - 1], code_recv.at[d - 1], seq=later(d))
 
@@ -201,8 +249,6 @@
     def _():
         for kv, (own, window) in enumerate(pairs):
             remote(own, window.at[0], own_send.at[kv], own_recv.at[kv], seq=partner).start()
-
-    slots = (3 - core, 2 - core)
 
     def pass_to_partner(i, kv, piece, order):
         window = pairs[kv][1]
@@ -232,11 +278,6 @@
             @pl.when(core == 0)
             def _():
                 arrive(here, pair_send.at[0, kv], pair_recv.at[0, kv, order])
-
-    last = n_z // 2
-
-    def active(way, step, i):
-        return step < last or (step == last and way == i)
 
     def ring_copy(way, step, i, kv):
         here = pairs[kv][1].at[slots[i], rows(turn(1 - step) if way == 0 else turn(step - 1))]
@@ -252,14 +293,12 @@
         for i in range(2):
             for kv in range(2):
                 for way in range(2):
-                    if not active(way, step, i):
-                        continue
                     piece = turn(-step) if way == 0 else turn(step)
                     here = pairs[kv][1].at[slots[i], rows(piece)]
                     arrive(here, ring_send.at[way, step - 1, i, kv], ring_recv.at[way, step - 1, i, kv])
-                    if active(way, step + 1, i):
+                    if step < last - 1:
                         ring_copy(way, step + 1, i, kv)
-                    pass_to_partner(i, kv, piece, 2 * step - 1 if step == last else 2 * step - 1 + way)
+                    pass_to_partner(i, kv, piece, 2 * step - 1 + way)
 
     code = c_ref[...].astype(F32)
     leading = code[:, :1]
@@ -283,18 +322,21 @@
         query_at = lax.broadcasted_iota(jnp.int32, (limit, TILE), 1) + start
         return same & (key_at <= query_at)
 
+    unit = (lax.broadcasted_iota(jnp.int32, (count, width), 1) == 0).astype(F32).astype(BF16)
+
     def own_tile(start):
         limit = start + TILE
         cols = slice(start, limit)
-        mask = own_mask(start, limit)
-        scores = dot(k_ref[:limit], q_ref[cols], 1, 1)
-        scores = jnp.where(mask, scores * factor, NEGATIVE)
-        top = jnp.max(scores, axis=0, keepdims=True)
-        weights = jnp.exp2(scores - top)
-        top_ref[:, cols] = top
-        sum_ref[:, cols] = jnp.sum(weights, axis=0, keepdims=True)
-        acc_ref[:, cols] = dot(vt_ref[:width, :limit], weights.astype(BF16), 1, 0)
-        products = jnp.where(mask, dot(kfb_ref[:limit], qft[:, cols], 1, 0), 0.0)
+        same = across(kcol_ref[cols], limit) == code[:, :limit]
+        key_at = lax.broadcasted_iota(jnp.int32, (TILE, limit), 1)
+        query_at = lax.broadcasted_iota(jnp.int32, (TILE, limit), 0) + start
+        scores = dot(q_ref[cols], k_ref[:limit], 1, 1)
+        scores = jnp.where(same & (key_at <= query_at), scores * factor, NEGATIVE)
+        top = jnp.broadcast_to(jnp.max(scores, axis=1, keepdims=True), (TILE, width))
+        weights = jnp.exp2(scores - across(top, limit)).astype(BF16)
+        top_ref[cols] = top
+        acc_ref[cols] = dot(weights, jnp.concatenate([v_ref[:limit], unit[:limit]], axis=1), 1, 0)
+        products = jnp.where(own_mask(start, limit), dot(kfb_ref[:limit], qft[:, cols], 1, 0), 0.0)
         den_ref[:, cols] = jnp.sum(products, axis=0, keepdims=True)
         num_ref[:, cols] = dot(vt_ref[:width, :limit], products.astype(BF16), 1, 0)
 
@@ -302,67 +344,74 @@
         places = [(d, rows(p), p) for d in range(REACH) for p in pieces]
         keys = jnp.concatenate([wk_ref[d, r] for d, r, _ in places], axis=0)
         vals = jnp.concatenate([wv_ref[d, r] for d, r, _ in places], axis=0)
-        column = jnp.concatenate([fcol_ref[d, r] for d, r, _ in places], axis=0)
-        shared = jnp.concatenate([wc_ref[d, :, rows(p)] for d, _, p in places], axis=1)
-        shared = (shared.astype(F32) == leading).astype(F32)
-        chosen = features(keys, wkey_t).astype(BF16).astype(F32) * shared
+        codes = jnp.concatenate([wc_ref[d, :, r] for d, r, _ in places], axis=1).astype(F32)
+        size = keys.shape[0]
+        feat = features(keys, wkey_t)
+        for n, (d, r, _) in enumerate(places):
+            fkf_ref[d, :, r] = feat[:, n * part : (n + 1) * part]
+        chosen = feat.astype(BF16).astype(F32) * (codes == leading).astype(F32)
         state_ref[...] += dot(chosen.astype(BF16), vals, 1, 0)
         ssum_ref[...] += jnp.broadcast_to(jnp.sum(chosen, axis=1, keepdims=True), ssum_ref.shape)
-        vals_t = transposed(vals)
+        wide = jnp.concatenate([vals, unit[:size]], axis=1)
         for start in range(0, count, TILE):
             cols = slice(start, start + TILE)
-            mask = across(column, TILE) == code[:, cols]
-            scores = dot(keys, q_ref[cols], 1, 1)
-            scores = jnp.where(mask, scores * factor, NEGATIVE)
-            old = top_ref[:, cols]
-            top = jnp.maximum(old, jnp.max(scores, axis=0, keepdims=True))
-            weights = jnp.exp2(scores - top)
+            scores = dot(q_ref[cols], keys, 1, 1)
+            same = across(kcol_ref[cols], size) == codes
+            scores = jnp.where(same, scores * factor, NEGATIVE)
+            old = top_ref[cols]
+            top = jnp.maximum(old, jnp.max(scores, axis=1, keepdims=True))
+            weights = jnp.exp2(scores - across(top, size)).astype(BF16)
             shrink = jnp.exp2(old - top)
-            top_ref[:, cols] = top
-            sum_ref[:, cols] = sum_ref[:, cols] * shrink + jnp.sum(weights, axis=0, keepdims=True)
-            acc_ref[:, cols] = acc_ref[:, cols] * shrink + dot(vals_t, weights.astype(BF16), 1, 0)
+            top_ref[cols] = top
+            acc_ref[cols] = acc_ref[cols] * across(shrink, 2 * width) + dot(weights, wide, 1, 0)
 
     for start in range(0, count // 2, TILE):
         own_tile(start)
-    for d in range(REACH):
-        arrive(wc_ref.at[d], code_send.at[d], code_recv.at[d])
-        fcol_ref[d] = lane_copies(wc_ref[d].astype(F32), width)
     state_ref[...] = jnp.zeros_like(state_ref)
     ssum_ref[...] = jnp.zeros_like(ssum_ref)
     for i in range(2):
         for kv in range(2):
-            here = pairs[kv][1].at[slots[i], rows(z)]
-            arrive(here, slice_send.at[0, kv], slice_recv.at[i, kv])
+            take_slice(0, i, kv)
             for way in range(2):
                 ring_copy(way, 1, i, kv)
             pass_to_partner(i, kv, z, 0)
+    send_slice(1)
     for start in range(count // 2, count, TILE):
         own_tile(start)
+    for d in range(REACH):
+        arrive(wc_ref.at[d], code_send.at[d], code_recv.at[d])
 
     @pl.when(core == 1)
     def _():
         for kv in range(2):
             arrive(pairs[kv][1].at[0], own_send.at[kv], own_recv.at[kv])
 
+    def both_from_partner(step):
+        from_partner(2 * step - 1, turn(-step))
+        from_partner(2 * step, turn(step))
+
     ring_step(1)
     from_partner(0, z)
     far_pieces((z,))
-    for step in range(1, last - 1):
-        ring_step(step + 1)
-        for way in range(2):
-            from_partner(2 * step - 1 + way, turn(-step) if way == 0 else turn(step))
-        far_pieces((turn(-step), turn(step)))
-    step = last - 1
-    for way in range(2):
-        from_partner(2 * step - 1 + way, turn(-step) if way == 0 else turn(step))
-    far_pieces((turn(-step), turn(step)))
-    ring_step(last)
-    from_partner(2 * last - 1, turn(last))
+    for i in range(2):
+        for kv in range(2):
+            take_slice(1, i, kv)
+            pass_to_partner(i, kv, turn(last), n_z - 1)
+    ring_step(2)
+    both_from_partner(1)
+    far_pieces((turn(-1), turn(1)))
+    from_partner(n_z - 1, turn(last))
     far_pieces((turn(last),))
+    ring_step(3)
+    both_from_partner(2)
+    far_pieces((turn(-2), turn(2)))
+    both_from_partner(3)
+    far_pieces((turn(-3), turn(3)))
 
     state = state_ref[...]
     state_sum = ssum_ref[:, :1]
-    teacher = acc_ref[...] / sum_ref[...]
+    acc = acc_ref[...]
+    teacher = (acc[:, :width] / acc[:, width : width + 1]).T
     numerator = num_ref[...] + lead * dot(state.T.astype(BF16), qft, 1, 0)
     denominator = den_ref[...] + lead * jnp.sum(
         qft.astype(F32) * state_sum, axis=0, keepdims=True
@@ -440,6 +489,20 @@
     grad_aq = features_back(qf_ref[...], gqf_ref[...]).astype(BF16)
     over_core(0, dot(grad_aq, q_ref[...], 1, 0))
     student_ref[...] = estimate.T.astype(BF16)
+    store = pltpu.make_async_copy(student_ref, student_hbm, store_sem.at[0])
+    store.start()
+
+    grad_ak = features_back(kf_ref[...], gkf_ref[...]).astype(BF16)
+    grad_wk = dot(grad_ak, k_ref[...], 1, 0)
+    adjoint_t = adjoint.T
+    adjoint_b = adjoint_t[:, :width].astype(BF16)
+    adjoint_sum = adjoint_t[:, width : width + 1]
+    for d in range(REACH):
+        met = (wc_ref[d].astype(F32) == leading).astype(F32)
+        caused = (dot(adjoint_b, wv_ref[d], 1, 1) + adjoint_sum) * met
+        grad_ak = features_back(fkf_ref[d], caused).astype(BF16)
+        grad_wk = grad_wk + dot(grad_ak, wk_ref[d], 1, 0)
+    over_core(1, grad_wk)
     over_y(0)
 
     final = code[:, count - 1 :]
@@ -449,6 +512,7 @@
         arrive(adj_in.at[d], adj_send.at[d], adj_recv.at[d])
         arrived = adj_in[d].astype(F32)
         entering = entering + jnp.where(arrived[width + 1 : width + 2] == final, arrived, 0.0)
+    over_y(1)
     added = dot(entering.T.astype(BF16), vt_ref[...], 1, 0)
     grad_kf = gkf_ref[...] + back * added
     spread_ref[...] = (grad_kf * total).astype(BF16)
@@ -463,16 +527,13 @@
         )
     gather_ref[0, z] = spread_ref[pl.ds(pl.multiple_of(z * share, share), share)]
 
-    grad_ak = features_back(kf_ref[...], grad_kf).astype(BF16)
-    over_core(1, dot(grad_ak, k_ref[...], 1, 0))
     over_x(0)
-    over_y(1)
-    gwq_out[...] = over_seq(0)
     over_x(1)
     z_ref[0, z] = over_seq(1).astype(BF16)
     here = z_ref.at[0, z]
     for i in range(1, n_z):
         send(here, here, z_send.at[0, i - 1], z_recv.at[0, z], tensor=turn(i))
+    gwq_out[...] = over_seq(0)
     for i in range(1, n_z):
         wait(gather_ref, 0, turn(i), spread_send, spread_recv)
     kfg_out[...] = summed(gather_ref, 0)
@@ -480,6 +541,7 @@
         wait(z_ref, 0, turn(i), z_send, z_recv)
     gwk_out[...] = summed(z_ref, 0)
 
+    store.wait()
     for copy in started:
         copy.wait_send()
     for kv, (own, window) in enumerate(pairs):
@@ -489,6 +551,10 @@
         @pl.when(core == 1)
         def _():
             remote(block, block, pair_send.at[0, kv], own_recv.at[kv], seq=partner).wait_send()
+            for j in range(2):
+                for i in range(2):
+                    here = window.at[0, rows(z)]
+                    remote(here, here, pass_send.at[j, i, kv], own_recv.at[kv], seq=partner).wait_send()
 
         @pl.when(core == 0)
         def _():
@@ -508,22 +574,31 @@
             jax.ShapeDtypeStruct((half, width), F32),
             jax.ShapeDtypeStruct((feat // n_z, count), F32),
         ),
-        in_specs=[pl.BlockSpec(memory_space=VMEM)] * 6,
-        out_specs=(pl.BlockSpec(memory_space=VMEM),) * 4,
+        in_specs=[pl.BlockSpec(memory_space=pl.ANY)] * 6,
+        out_specs=(
+            pl.BlockSpec(memory_space=pl.ANY),
+            *[pl.BlockSpec(memory_space=VMEM)] * 3,
+        ),
         scratch_shapes=[
+            VMEM((count, width), BF16),
+            VMEM((count, width), BF16),
+            VMEM((count, width), BF16),
+            VMEM((1, count), jnp.int32),
+            VMEM((half, width), BF16),
+            VMEM((half, width), BF16),
+            VMEM((count, width), BF16),
             VMEM((REACH, count, width), BF16),
             VMEM((REACH, count, width), BF16),
             VMEM((REACH, 1, count), jnp.int32),
             VMEM((count, width), F32),
-            VMEM((REACH, count, width), F32),
+            VMEM((REACH, feat, count), F32),
             VMEM((ADJ_ROWS, count), BF16),
             VMEM((count, feat), BF16),
             VMEM((feat, count), F32),
             VMEM((feat, count), F32),
+            VMEM((count, width), F32),
             VMEM((1, count), F32),
-            VMEM((1, count), F32),
-            VMEM((1, count), F32),
-            VMEM((width, count), F32),
+            VMEM((count, 2 * width), F32),
             VMEM((width, count), F32),
             VMEM((feat, width), F32),
             VMEM((feat, width), F32),
@@ -537,14 +612,17 @@
             VMEM((2, SIDE, half, width), BF16),
             VMEM((2, SIDE, half, width), BF16),
             VMEM((1, n_z, half, width), BF16),
+            dma((6,)),
+            dma((1,)),
             dma((REACH,)),
             dma((REACH,)),
             dma((2, 2)),
-            dma((2, 2)),
+            dma((2, 2, 2)),
+            dma((2, 2, 2)),
             dma((2,)),
             dma((2,)),
-            dma((2, n_z // 2, 2, 2)),
-            dma((2, n_z // 2, 2, 2)),
+            dma((2, n_z // 2 - 1, 2, 2)),
+            dma((2, n_z // 2 - 1, 2, 2)),
             dma((2, 2)),
             dma((2, 2, n_z)),
             dma((REACH,)),

time: 66.6 us -> 58.9 us (0.88)
  Pallas kernels: 62 us -> 53.7 us
    pallas_call x1, Pallas kernels: 62 us -> 53.7 us  [fused(): pl.pallas_call(functools.partial(fused_kernel, n_seq, n_z), out_shape=(ja...]
where the time goes in v3:
time: 58.9 us; the launch traced here: 57.9 us
  Pallas kernels  53.7 us (91%)
  local copies, waits for them, and re-layouts  3.55 us (6%)
  between operations  0.66 us (1%)
    pallas_call x1, Pallas kernels, fused(): pl.pallas_call(functools.partial(fused_kernel, n_seq, n_z), out_shape=(ja...  53.7 us
    unnamed x10, local copies, waits for them, and re-layouts  3.55 us

profile of v3, /device:TPU:1, one launch (start us, length us, event | category | flops | bytes accessed | tf_op | source)
XLA Modules:
  0.0 57.9 jit_solution(12467102008979463887)
XLA Ops:
  0.6 53.7 %fused.1 = (bf16[1024,128]{1,0:T(8,128)(2,1)}, f32[64,128]{1,0:T(8,128)}, f32[64,128]{1,0:T(8,128)}, f32[16,1024]{1,0:T(8,128)}) custom-call(bf16[1024,128]{1,0:T(8,128)(2,1)} %bitcast.12, bf16[1024,128]{1,0:T(8,128)(2,1)} %k_hbm.1, bf16[1024,128]{1,0:T(8,128)(2,1)} %v_hbm.1, s32[1,1024]{1,0:T(1,128)} %bitcast.19, bf16[64,128]{1,0:T(8,128)(2,1)} %bitcast.17, ...), custom_call_target="tpu_custom_call" | custom-call | tf_op jit(solution)/shard_map/fused/pallas_call | solution.py:569
  54.3 0.0 copy-start.2
  54.3 0.0 copy-start.1
  54.3 1.7 %copy.14 = bf16[1024,1,128]{2,0,1:T(8,128)(2,1)} copy(bf16[1024,1,128]{2,0,1:T(8,128)(2,1)} %bitcast.13) | data formatting | bytes 524288
  56.0 0.0 copy-done.2
  56.0 0.0 copy-start
  56.0 0.6 %copy.15 = f32[1,128,64]{1,2,0:T(8,128)} copy(f32[1,128,64]{1,2,0:T(8,128)S(1)} %bitcast.16) | data formatting | bytes 65536
  56.6 0.0 copy-done.1
  56.6 0.6 %copy.16 = f32[128,64]{0,1:T(8,128)} copy(f32[128,64]{0,1:T(8,128)S(1)} %bitcast.15) | data formatting | bytes 65536
  57.3 0.0 copy-done
  57.3 0.6 %copy.17 = f32[1024,16]{0,1:T(8,128)} copy(f32[1024,16]{0,1:T(8,128)S(1)} %bitcast.14) | data formatting | bytes 131072
Async XLA Ops:
  54.3 1.7 %copy-start.2 = (f32[64,128]{1,0:T(8,128)S(1)}, f32[64,128]{1,0:T(8,128)}, u32[]{:S(2)}) copy-start(f32[64,128]{1,0:T(8,128)} %get-tuple-element.9) | copy-start | bytes 98308
  54.3 2.3 %copy-start.1 = (f32[64,128]{1,0:T(8,128)S(1)}, f32[64,128]{1,0:T(8,128)}, u32[]{:S(2)}) copy-start(f32[64,128]{1,0:T(8,128)} %get-tuple-element.10) | copy-start | bytes 98308
  56.0 1.2 %copy-start = (f32[16,1024]{1,0:T(8,128)S(1)}, f32[16,1024]{1,0:T(8,128)}, u32[]{:S(2)}) copy-start(f32[16,1024]{1,0:T(8,128)} %get-tuple-element.11) | copy-start | bytes 196612

commit v4 on v3

--- a/solution.py
+++ b/solution.py
@@ -197,7 +197,7 @@
         signal(barrier, seq=seq_of(along_x(i), y))
     for i in range(1, n_z):
         signal(barrier, tensor=turn(i))
-    for load in loads:
+    for load in loads[:3]:
         load.wait()
     pl.semaphore_wait(barrier, 2 * REACH + 1 + 2 * (SIDE - 1) + n_z - 1)
 
@@ -214,7 +214,7 @@
     pairs = ((k_ref, wk_ref), (v_ref, wv_ref))
     slots = (3 - core, 2 - core)
     last = n_z // 2
-    direct = (z, turn(last))
+    direct = (z, turn(last), turn(last - 1), turn(1 - last))
 
     def send_slice(j):
         for kv, (own, window) in enumerate(pairs):
@@ -242,6 +242,7 @@
             ).start()
 
     send_slice(0)
+    send_slice(1)
     for d in range(1, REACH + 1):
         send(c_ref, wc_ref.at[d - 1], code_send.at[d - 1], code_recv.at[d - 1], seq=later(d))
 
@@ -296,10 +297,12 @@
                     piece = turn(-step) if way == 0 else turn(step)
                     here = pairs[kv][1].at[slots[i], rows(piece)]
                     arrive(here, ring_send.at[way, step - 1, i, kv], ring_recv.at[way, step - 1, i, kv])
-                    if step < last - 1:
+                    if step < last - 2:
                         ring_copy(way, step + 1, i, kv)
                     pass_to_partner(i, kv, piece, 2 * step - 1 + way)
 
+    for load in loads[3:]:
+        load.wait()
     code = c_ref[...].astype(F32)
     leading = code[:, :1]
     lead = (code == leading).astype(F32)
@@ -375,7 +378,7 @@
             for way in range(2):
                 ring_copy(way, 1, i, kv)
             pass_to_partner(i, kv, z, 0)
-    send_slice(1)
+    send_slice(2)
     for start in range(count // 2, count, TILE):
         own_tile(start)
     for d in range(REACH):
@@ -390,19 +393,24 @@
         from_partner(2 * step - 1, turn(-step))
         from_partner(2 * step, turn(step))
 
+    def take_direct(j, order):
+        for i in range(2):
+            for kv in range(2):
+                take_slice(j, i, kv)
+                pass_to_partner(i, kv, direct[j], order)
+
+    take_direct(1, n_z - 1)
+    send_slice(3)
     ring_step(1)
     from_partner(0, z)
     far_pieces((z,))
-    for i in range(2):
-        for kv in range(2):
-            take_slice(1, i, kv)
-            pass_to_partner(i, kv, turn(last), n_z - 1)
+    take_direct(2, n_z - 2)
+    from_partner(n_z - 1, turn(last))
+    far_pieces((turn(last),))
     ring_step(2)
     both_from_partner(1)
     far_pieces((turn(-1), turn(1)))
-    from_partner(n_z - 1, turn(last))
-    far_pieces((turn(last),))
-    ring_step(3)
+    take_direct(3, n_z - 3)
     both_from_partner(2)
     far_pieces((turn(-2), turn(2)))
     both_from_partner(3)
@@ -486,12 +494,6 @@
             wait(x_ref, which, along_x(i), x_send, x_recv)
         return summed(x_ref, which)
 
-    grad_aq = features_back(qf_ref[...], gqf_ref[...]).astype(BF16)
-    over_core(0, dot(grad_aq, q_ref[...], 1, 0))
-    student_ref[...] = estimate.T.astype(BF16)
-    store = pltpu.make_async_copy(student_ref, student_hbm, store_sem.at[0])
-    store.start()
-
     grad_ak = features_back(kf_ref[...], gkf_ref[...]).astype(BF16)
     grad_wk = dot(grad_ak, k_ref[...], 1, 0)
     adjoint_t = adjoint.T
@@ -503,7 +505,13 @@
         grad_ak = features_back(fkf_ref[d], caused).astype(BF16)
         grad_wk = grad_wk + dot(grad_ak, wk_ref[d], 1, 0)
     over_core(1, grad_wk)
-    over_y(0)
+
+    grad_aq = features_back(qf_ref[...], gqf_ref[...]).astype(BF16)
+    over_core(0, dot(grad_aq, q_ref[...], 1, 0))
+    student_ref[...] = estimate.T.astype(BF16)
+    store = pltpu.make_async_copy(student_ref, student_hbm, store_sem.at[0])
+    store.start()
+    over_y(1)
 
     final = code[:, count - 1 :]
     back = (code == final).astype(F32)
@@ -512,7 +520,6 @@
         arrive(adj_in.at[d], adj_send.at[d], adj_recv.at[d])
         arrived = adj_in[d].astype(F32)
         entering = entering + jnp.where(arrived[width + 1 : width + 2] == final, arrived, 0.0)
-    over_y(1)
     added = dot(entering.T.astype(BF16), vt_ref[...], 1, 0)
     grad_kf = gkf_ref[...] + back * added
     spread_ref[...] = (grad_kf * total).astype(BF16)
@@ -527,12 +534,13 @@
         )
     gather_ref[0, z] = spread_ref[pl.ds(pl.multiple_of(z * share, share), share)]
 
-    over_x(0)
     over_x(1)
+    over_y(0)
     z_ref[0, z] = over_seq(1).astype(BF16)
     here = z_ref.at[0, z]
     for i in range(1, n_z):
         send(here, here, z_send.at[0, i - 1], z_recv.at[0, z], tensor=turn(i))
+    over_x(0)
     gwq_out[...] = over_seq(0)
     for i in range(1, n_z):
         wait(gather_ref, 0, turn(i), spread_send, spread_recv)
@@ -551,7 +559,7 @@
         @pl.when(core == 1)
         def _():
             remote(block, block, pair_send.at[0, kv], own_recv.at[kv], seq=partner).wait_send()
-            for j in range(2):
+            for j in range(len(direct)):
                 for i in range(2):
                     here = window.at[0, rows(z)]
                     remote(here, here, pass_send.at[j, i, kv], own_recv.at[kv], seq=partner).wait_send()
@@ -616,13 +624,13 @@
             dma((1,)),
             dma((REACH,)),
             dma((REACH,)),
-            dma((2, 2)),
-            dma((2, 2, 2)),
-            dma((2, 2, 2)),
+            dma((4, 2)),
+            dma((4, 2, 2)),
+            dma((4, 2, 2)),
             dma((2,)),
             dma((2,)),
-            dma((2, n_z // 2 - 1, 2, 2)),
-            dma((2, n_z // 2 - 1, 2, 2)),
+            dma((2, n_z // 2 - 2, 2, 2)),
+            dma((2, n_z // 2 - 2, 2, 2)),
             dma((2, 2)),
             dma((2, 2, n_z)),
             dma((REACH,)),
@@ -643,20 +651,38 @@
     )(queries, keys, values, codes, wq_t, wkey_t)
 
 
+def publish_kernel(*refs):
+    half = len(refs) // 2
+    for given, out in zip(refs[:half], refs[half:]):
+        out[...] = given[...]
+
+
+def publish(*results):
+    return pl.pallas_call(
+        publish_kernel,
+        out_shape=tuple(jax.ShapeDtypeStruct(r.shape, r.dtype) for r in results),
+        in_specs=[pl.BlockSpec(memory_space=VMEM)] * len(results),
+        out_specs=(pl.BlockSpec(memory_space=VMEM),) * len(results),
+        name="publish",
+    )(*results)
+
+
 def solution(mesh):
     n_seq, n_z = mesh.shape["seq"], mesh.shape["tensor"]
 
     def shards(queries, keys, values, doc_ids, w_query, w_key):
         count, width = keys.shape
-        student, gwq, gwk, kfg = fused(
-            queries.reshape(count, width),
-            keys,
-            values,
-            doc_ids.reshape(1, count),
-            w_query[0].T,
-            w_key.T,
-            n_seq,
-            n_z,
+        student, gwq, gwk, kfg = publish(
+            *fused(
+                queries.reshape(count, width),
+                keys,
+                values,
+                doc_ids.reshape(1, count),
+                w_query[0].T,
+                w_key.T,
+                n_seq,
+                n_z,
+            )
         )
         return student.reshape(queries.shape), gwq.T[None], gwk.T, kfg.T
 

time: 58.9 us -> 54.6 us (0.927); the launches traced: 57.9 us -> 54.3 us
  local copies, waits for them, and re-layouts: 3.55 us -> 0 us
    unnamed x10 -> x0, local copies, waits for them, and re-layouts: 3.55 us -> none
    pallas_call x1, Pallas kernels: 53.7 us -> 51.9 us  [fused(): pl.pallas_call(functools.partial(fused_kernel, n_seq, n_z), out_shape=(ja...]
    pallas_call x0 -> x1, Pallas kernels: none -> 1.72 us  [publish(): pl.pallas_call(publish_kernel, out_shape=tuple((jax.ShapeDtypeStruct(r.sh...]
where the time goes in v4:
time: 54.6 us; the launch traced here: 54.3 us
  Pallas kernels  53.6 us (98%)
  between operations  0.64 us (1%)
    pallas_call x1, Pallas kernels, fused(): pl.pallas_call(functools.partial(fused_kernel, n_seq, n_z), out_shape=(ja...  51.9 us
    pallas_call x1, Pallas kernels, publish(): pl.pallas_call(publish_kernel, out_shape=tuple((jax.ShapeDtypeStruct(r.sh...  1.72 us

profile of v4, /device:TPU:1, one launch (start us, length us, event | category | flops | bytes accessed | tf_op | source)
XLA Modules:
  0.0 54.3 jit_solution(15931745988446757831)
XLA Ops:
  0.6 51.9 %fused.1 = (bf16[1024,128]{1,0:T(8,128)(2,1)}, f32[64,128]{1,0:T(8,128)}, f32[64,128]{1,0:T(8,128)}, f32[16,1024]{1,0:T(8,128)}) custom-call(bf16[1024,128]{1,0:T(8,128)(2,1)} %bitcast.12, bf16[1024,128]{1,0:T(8,128)(2,1)} %k_hbm.1, bf16[1024,128]{1,0:T(8,128)(2,1)} %v_hbm.1, s32[1,1024]{1,0:T(1,128)} %bitcast.15, bf16[64,128]{1,0:T(8,128)(2,1)} %bitcast.13, ...), custom_call_target="tpu_custom_call" | custom-call | tf_op jit(solution)/shard_map/fused/pallas_call | solution.py:577
  52.6 1.7 %publish.1 = (bf16[1024,128]{1,0:T(8,128)(2,1)}, f32[64,128]{1,0:T(8,128)}, f32[64,128]{1,0:T(8,128)}, f32[16,1024]{1,0:T(8,128)}) custom-call(bf16[1024,128]{1,0:T(8,128)(2,1)} %get-tuple-element.12.refs_0_, f32[64,128]{1,0:T(8,128)} %get-tuple-element.13.refs_1_, f32[64,128]{1,0:T(8,128)} %get-tuple-element.14.refs_2_, f32[16,1024]{1,0:T(8,128)} %get-tuple-element.15.refs_3_), custom_call_target="tpu_custom_call" | custom-call | tf_op jit(solution)/shard_map/publish/pallas_call | solution.py:661

commit v5 on v4

--- a/solution.py
+++ b/solution.py
@@ -212,37 +212,21 @@
         remote(here, here, send_sem, recv_sem, seq=partner).wait_recv()
 
     pairs = ((k_ref, wk_ref), (v_ref, wv_ref))
-    slots = (3 - core, 2 - core)
     last = n_z // 2
     direct = (z, turn(last), turn(last - 1), turn(1 - last))
 
-    def send_slice(j):
+    def send_slice(j, at):
         for kv, (own, window) in enumerate(pairs):
-            send(
+            remote(
                 own.at[rows(direct[j])],
-                window.at[2 - core, rows(direct[j])],
+                window.at[2 - at, rows(direct[j])],
                 slice_send.at[j, kv],
-                slice_recv.at[j, core, kv],
-                seq=later(3 - core),
-            )
-
-    def take_slice(j, i, kv):
-        window = pairs[kv][1]
-        here = window.at[slots[i], rows(direct[j])]
-        arrive(here, slice_send.at[j, kv], slice_recv.at[j, i, kv])
-
-        @pl.when(core == 1)
-        def _():
-            remote(
-                here,
-                window.at[3 - i, rows(direct[j])],
-                pass_send.at[j, i, kv],
-                slice_recv.at[j, i, kv],
-                seq=later(1),
+                slice_recv.at[j, at, kv],
+                seq=later(3 - at),
             ).start()
 
-    send_slice(0)
-    send_slice(1)
+    for j in range(2):
+        send_slice(j, core)
     for d in range(1, REACH + 1):
         send(c_ref, wc_ref.at[d - 1], code_send.at[d - 1], code_recv.at[d - 1], seq=later(d))
 
@@ -251,55 +235,67 @@
         for kv, (own, window) in enumerate(pairs):
             remote(own, window.at[0], own_send.at[kv], own_recv.at[kv], seq=partner).start()
 
-    def pass_to_partner(i, kv, piece, order):
+    def pass_to_partner(at, i, kv, piece, order):
+        if at == 0 and i == 0:
+            return
         window = pairs[kv][1]
-
-        def go(slot):
-            remote(
-                window.at[slots[i], rows(piece)],
-                window.at[slot, rows(piece)],
-                pair_send.at[i, kv],
-                pair_recv.at[i, kv, order],
-                seq=partner,
-            ).start()
-
-        if i == 1:
-            go(3 - 3 * core)
-        else:
-
-            @pl.when(core == 1)
-            def _():
-                go(1)
-
-    def from_partner(order, piece):
-        for kv in range(2):
-            here = pairs[kv][1].at[0, rows(piece)]
-            arrive(here, pair_send.at[1, kv], pair_recv.at[1, kv, order])
-
-            @pl.when(core == 0)
-            def _():
-                arrive(here, pair_send.at[0, kv], pair_recv.at[0, kv, order])
-
-    def ring_copy(way, step, i, kv):
-        here = pairs[kv][1].at[slots[i], rows(turn(1 - step) if way == 0 else turn(step - 1))]
-        send(
+        remote(
+            window.at[3 - at - i, rows(piece)],
+            window.at[3 if at == 0 else 1 - i, rows(piece)],
+            pair_send.at[i, kv],
+            pair_recv.at[i, kv, order],
+            seq=partner,
+        ).start()
+
+    def from_partner(at, *orders):
+        for order in orders:
+            here = rows(turn(order_turn[order]))
+            for kv in range(2):
+                for i in range(at, 2):
+                    arrive(pairs[kv][1].at[0, here], pair_send.at[i, kv], pair_recv.at[i, kv, order])
+
+    order_turn = (0, -1, 1, -2, 2, -3, 3, last)
+
+    def take_slice(at, j, order):
+        for i in range(2):
+            for kv in range(2):
+                window = pairs[kv][1]
+                here = window.at[3 - at - i, rows(direct[j])]
+                arrive(here, slice_send.at[j, kv], slice_recv.at[j, i, kv])
+                if j == 0:
+                    for way in range(2):
+                        ring_copy(at, way, 1, i, kv)
+                if at == 1:
+                    remote(
+                        here,
+                        window.at[3 - i, rows(direct[j])],
+                        pass_send.at[j, i, kv],
+                        slice_recv.at[j, i, kv],
+                        seq=later(1),
+                    ).start()
+                pass_to_partner(at, i, kv, direct[j], order)
+
+    def ring_copy(at, way, step, i, kv):
+        piece = rows(turn(1 - step) if way == 0 else turn(step - 1))
+        here = pairs[kv][1].at[3 - at - i, piece]
+        remote(
             here,
             here,
             ring_send.at[way, step - 1, i, kv],
             ring_recv.at[way, step - 1, i, kv],
             tensor=turn(1 if way == 0 else -1),
-        )
-
-    def ring_step(step):
+        ).start()
+
+    def ring_step(at, step):
         for i in range(2):
             for kv in range(2):
                 for way in range(2):
                     piece = turn(-step) if way == 0 else turn(step)
-                    here = pairs[kv][1].at[slots[i], rows(piece)]
+                    here = pairs[kv][1].at[3 - at - i, rows(piece)]
                     arrive(here, ring_send.at[way, step - 1, i, kv], ring_recv.at[way, step - 1, i, kv])
                     if step < last - 2:
-                        ring_copy(way, step + 1, i, kv)
-                    pass_to_partner(i, kv, piece, 2 * step - 1 + way)
+                        ring_copy(at, way, step + 1, i, kv)
+                    pass_to_partner(at, i, kv, piece, 2 * step - 1 + way)
 
     for load in loads[3:]:
         load.wait()
@@ -343,14 +339,14 @@
         den_ref[:, cols] = jnp.sum(products, axis=0, keepdims=True)
         num_ref[:, cols] = dot(vt_ref[:width, :limit], products.astype(BF16), 1, 0)
 
-    def far_pieces(pieces):
-        places = [(d, rows(p), p) for d in range(REACH) for p in pieces]
-        keys = jnp.concatenate([wk_ref[d, r] for d, r, _ in places], axis=0)
-        vals = jnp.concatenate([wv_ref[d, r] for d, r, _ in places], axis=0)
-        codes = jnp.concatenate([wc_ref[d, :, r] for d, r, _ in places], axis=1).astype(F32)
+    def far_pieces(blocks, *orders):
+        places = [(d, rows(turn(order_turn[n]))) for d in blocks for n in orders]
+        keys = jnp.concatenate([wk_ref[d, r] for d, r in places], axis=0)
+        vals = jnp.concatenate([wv_ref[d, r] for d, r in places], axis=0)
+        codes = jnp.concatenate([wc_ref[d, :, r] for d, r in places], axis=1).astype(F32)
         size = keys.shape[0]
         feat = features(keys, wkey_t)
-        for n, (d, r, _) in enumerate(places):
+        for n, (d, r) in enumerate(places):
             fkf_ref[d, :, r] = feat[:, n * part : (n + 1) * part]
         chosen = feat.astype(BF16).astype(F32) * (codes == leading).astype(F32)
         state_ref[...] += dot(chosen.astype(BF16), vals, 1, 0)
@@ -368,53 +364,63 @@
             top_ref[cols] = top
             acc_ref[cols] = acc_ref[cols] * across(shrink, 2 * width) + dot(weights, wide, 1, 0)
 
-    for start in range(0, count // 2, TILE):
-        own_tile(start)
+    def own_tiles(first, end):
+        for start in range(first, end, TILE):
+            own_tile(start)
+
+    def codes_arrive():
+        for d in range(REACH):
+            arrive(wc_ref.at[d], code_send.at[d], code_recv.at[d])
+
     state_ref[...] = jnp.zeros_like(state_ref)
     ssum_ref[...] = jnp.zeros_like(ssum_ref)
-    for i in range(2):
-        for kv in range(2):
-            take_slice(0, i, kv)
-            for way in range(2):
-                ring_copy(way, 1, i, kv)
-            pass_to_partner(i, kv, z, 0)
-    send_slice(2)
-    for start in range(count // 2, count, TILE):
-        own_tile(start)
-    for d in range(REACH):
-        arrive(wc_ref.at[d], code_send.at[d], code_recv.at[d])
 
     @pl.when(core == 1)
     def _():
+        own_tiles(0, count // 2)
+        take_slice(1, 0, 0)
+        send_slice(2, 1)
+        own_tiles(count // 2, count)
+        take_slice(1, 1, 7)
+        send_slice(3, 1)
+        codes_arrive()
         for kv in range(2):
             arrive(pairs[kv][1].at[0], own_send.at[kv], own_recv.at[kv])
-
-    def both_from_partner(step):
-        from_partner(2 * step - 1, turn(-step))
-        from_partner(2 * step, turn(step))
-
-    def take_direct(j, order):
-        for i in range(2):
-            for kv in range(2):
-                take_slice(j, i, kv)
-                pass_to_partner(i, kv, direct[j], order)
-
-    take_direct(1, n_z - 1)
-    send_slice(3)
-    ring_step(1)
-    from_partner(0, z)
-    far_pieces((z,))
-    take_direct(2, n_z - 2)
-    from_partner(n_z - 1, turn(last))
-    far_pieces((turn(last),))
-    ring_step(2)
-    both_from_partner(1)
-    far_pieces((turn(-1), turn(1)))
-    take_direct(3, n_z - 3)
-    both_from_partner(2)
-    far_pieces((turn(-2), turn(2)))
-    both_from_partner(3)
-    far_pieces((turn(-3), turn(3)))
+        ring_step(1, 1)
+        far_pieces((0,), 0, 1, 2, 3)
+        take_slice(1, 2, 6)
+        far_pieces((1, 2), 0, 1, 2, 7)
+        ring_step(1, 2)
+        take_slice(1, 3, 5)
+        far_pieces((0,), 4, 5, 6, 7)
+        far_pieces((1, 2), 3, 4, 5, 6)
+        from_partner(1, 0, 1, 2, 7)
+        far_pieces((3,), 0, 1, 2, 7)
+        from_partner(1, 3, 4, 5, 6)
+        far_pieces((3,), 3, 4, 5, 6)
+
+    @pl.when(core == 0)
+    def _():
+        own_tiles(0, count // 2)
+        send_slice(2, 0)
+        own_tiles(count // 2, count)
+        send_slice(3, 0)
+        codes_arrive()
+        from_partner(0, 0, 7)
+        take_slice(0, 0, 0)
+        far_pieces((0, 1), 0, 7)
+        take_slice(0, 1, 7)
+        ring_step(0, 1)
+        from_partner(0, 1, 2)
+        far_pieces((0, 1), 1, 2)
+        take_slice(0, 2, 6)
+        far_pieces((2, 3), 0, 7)
+        ring_step(0, 2)
+        from_partner(0, 3, 4, 5, 6)
+        far_pieces((2, 3), 1, 2)
+        take_slice(0, 3, 5)
+        far_pieces((0, 1), 3, 4, 5, 6)
+        far_pieces((2, 3), 3, 4, 5, 6)
 
     state = state_ref[...]
     state_sum = ssum_ref[:, :1]
@@ -554,6 +560,15 @@
         copy.wait_send()
     for kv, (own, window) in enumerate(pairs):
         block = window.at[0]
+        here = window.at[0, rows(z)]
+        for j in range(len(direct)):
+            remote(here, here, slice_send.at[j, kv], own_recv.at[kv], seq=partner).wait_send()
+        for way in range(2):
+            for step in range(last - 2):
+                for i in range(2):
+                    remote(
+                        here, here, ring_send.at[way, step, i, kv], own_recv.at[kv], seq=partner
+                    ).wait_send()
         remote(block, block, pair_send.at[1, kv], own_recv.at[kv], seq=partner).wait_send()
 
         @pl.when(core == 1)
@@ -561,7 +576,6 @@
             remote(block, block, pair_send.at[0, kv], own_recv.at[kv], seq=partner).wait_send()
             for j in range(len(direct)):
                 for i in range(2):
-                    here = window.at[0, rows(z)]
                     remote(here, here, pass_send.at[j, i, kv], own_recv.at[kv], seq=partner).wait_send()
 
         @pl.when(core == 0)

time: 54.6 us -> 52.9 us (0.969)
  Pallas kernels: 53.6 us -> 52.1 us
    pallas_call x1, Pallas kernels: 51.9 us -> 50.4 us  [fused(): pl.pallas_call(functools.partial(fused_kernel, n_seq, n_z), out_shape=(ja...]
where the time goes in v5:
time: 52.9 us; the launch traced here: 52.8 us
  Pallas kernels  52.1 us (98%)
  between operations  0.64 us (1%)
    pallas_call x1, Pallas kernels, fused(): pl.pallas_call(functools.partial(fused_kernel, n_seq, n_z), out_shape=(ja...  50.4 us
    pallas_call x1, Pallas kernels, publish(): pl.pallas_call(publish_kernel, out_shape=tuple((jax.ShapeDtypeStruct(r.sh...  1.72 us

profile of v5, /device:TPU:1, one launch (start us, length us, event | category | flops | bytes accessed | tf_op | source)
XLA Modules:
  0.0 52.8 jit_solution(771141667289762639)
XLA Ops:
  0.6 50.4 %fused.1 = (bf16[1024,128]{1,0:T(8,128)(2,1)}, f32[64,128]{1,0:T(8,128)}, f32[64,128]{1,0:T(8,128)}, f32[16,1024]{1,0:T(8,128)}) custom-call(bf16[1024,128]{1,0:T(8,128)(2,1)} %bitcast.12, bf16[1024,128]{1,0:T(8,128)(2,1)} %k_hbm.1, bf16[1024,128]{1,0:T(8,128)(2,1)} %v_hbm.1, s32[1,1024]{1,0:T(1,128)} %bitcast.15, bf16[64,128]{1,0:T(8,128)(2,1)} %bitcast.13, ...), custom_call_target="tpu_custom_call" | custom-call | tf_op jit(solution)/shard_map/fused/pallas_call | solution.py:591
  51.1 1.7 %publish.1 = (bf16[1024,128]{1,0:T(8,128)(2,1)}, f32[64,128]{1,0:T(8,128)}, f32[64,128]{1,0:T(8,128)}, f32[16,1024]{1,0:T(8,128)}) custom-call(bf16[1024,128]{1,0:T(8,128)(2,1)} %get-tuple-element.12.refs_0_, f32[64,128]{1,0:T(8,128)} %get-tuple-element.13.refs_1_, f32[64,128]{1,0:T(8,128)} %get-tuple-element.14.refs_2_, f32[16,1024]{1,0:T(8,128)} %get-tuple-element.15.refs_3_), custom_call_target="tpu_custom_call" | custom-call | tf_op jit(solution)/shard_map/publish/pallas_call | solution.py:675

commit v6 on v5

--- a/solution.py
+++ b/solution.py
@@ -109,8 +109,7 @@
     adj_in,
     spread_ref,
     gather_ref,
-    core_ref,
-    y_ref,
+    row_ref,
     x_ref,
     z_ref,
     load_sem,
@@ -130,10 +129,8 @@
     adj_recv,
     spread_send,
     spread_recv,
-    core_send,
-    core_recv,
-    y_send,
-    y_recv,
+    row_send,
+    row_recv,
     x_send,
     x_recv,
     z_send,
@@ -148,8 +145,9 @@
     z = lax.axis_index("tensor")
     core = lax.rem(s, 2)
     partner = s + 1 - 2 * core
-    y = lax.rem(s // 2, SIDE)
-    x = s // (2 * SIDE)
+    row = 2 * SIDE
+    at_row = lax.rem(s, row)
+    x = s // row
     part = count // n_z
     share = 2 * half // n_z
 
@@ -159,14 +157,14 @@
     def turn(d):
         return lax.rem(z + d + n_z, n_z)
 
-    def along_y(i):
-        return lax.rem(y + i, SIDE)
+    def along_row(i):
+        return lax.rem(at_row + i, row)
 
     def along_x(i):
         return lax.rem(x + i, SIDE)
 
-    def seq_of(at_x, at_y):
-        return (at_x * SIDE + at_y) * 2 + core
+    def seq_of(to_x, to_row):
+        return to_x * row + to_row
 
     def rows(p):
         return pl.ds(pl.multiple_of(p * part, part), part)
@@ -191,15 +189,15 @@
     for d in range(1, REACH + 1):
         signal(barrier, seq=later(n_seq - d))
         signal(barrier, seq=later(d))
-    signal(barrier, seq=partner)
+    for i in range(1, row):
+        signal(barrier, seq=seq_of(x, along_row(i)))
     for i in range(1, SIDE):
-        signal(barrier, seq=seq_of(x, along_y(i)))
-        signal(barrier, seq=seq_of(along_x(i), y))
+        signal(barrier, seq=seq_of(along_x(i), at_row))
     for i in range(1, n_z):
         signal(barrier, tensor=turn(i))
     for load in loads[:3]:
         load.wait()
-    pl.semaphore_wait(barrier, 2 * REACH + 1 + 2 * (SIDE - 1) + n_z - 1)
+    pl.semaphore_wait(barrier, 2 * REACH + row - 1 + SIDE - 1 + n_z - 1)
 
     started = []
 
@@ -436,8 +434,8 @@
     grad_den = -jnp.sum(grad_out * estimate, axis=0, keepdims=True) / denominator
     gnt = grad_num.astype(BF16)
 
-    row = lax.broadcasted_iota(jnp.int32, (ADJ_ROWS - width, count), 0)
-    tail = jnp.where(row == 0, grad_den * lead, 0.0)
+    line = lax.broadcasted_iota(jnp.int32, (ADJ_ROWS - width, count), 0)
+    tail = jnp.where(line == 0, grad_den * lead, 0.0)
     masked = jnp.concatenate([grad_num * lead, tail], axis=0).astype(BF16)
     adjoint = dot(masked, qft, 1, 1)
     mark = lax.broadcasted_iota(jnp.int32, adjoint.shape, 0)
@@ -473,26 +471,20 @@
             result = result + ref[which, i].astype(F32)
         return result
 
-    def over_core(which, value):
-        core_ref[which, core] = value.astype(BF16)
-        here = core_ref.at[which, core]
-        send(here, here, core_send.at[which, 0], core_recv.at[which, core], seq=partner)
-
-    def over_y(which):
-        wait(core_ref, which, 1 - core, core_send, core_recv)
-        y_ref[which, y] = summed(core_ref, which).astype(BF16)
-        here = y_ref.at[which, y]
-        for i in range(1, SIDE):
-            to = seq_of(x, along_y(i))
-            send(here, here, y_send.at[which, i - 1], y_recv.at[which, y], seq=to)
+    def over_row(which, value):
+        row_ref[which, at_row] = value.astype(BF16)
+        here = row_ref.at[which, at_row]
+        for i in range(1, row):
+            to = seq_of(x, along_row(i))
+            send(here, here, row_send.at[which, i - 1], row_recv.at[which, at_row], seq=to)
 
     def over_x(which):
-        for i in range(1, SIDE):
-            wait(y_ref, which, along_y(i), y_send, y_recv)
-        x_ref[which, x] = summed(y_ref, which).astype(BF16)
+        for i in range(1, row):
+            wait(row_ref, which, along_row(i), row_send, row_recv)
+        x_ref[which, x] = summed(row_ref, which).astype(BF16)
         here = x_ref.at[which, x]
         for i in range(1, SIDE):
-            to = seq_of(along_x(i), y)
+            to = seq_of(along_x(i), at_row)
             send(here, here, x_send.at[which, i - 1], x_recv.at[which, x], seq=to)
 
     def over_seq(which):
@@ -510,14 +502,13 @@
         caused = (dot(adjoint_b, wv_ref[d], 1, 1) + adjoint_sum) * met
         grad_ak = features_back(fkf_ref[d], caused).astype(BF16)
         grad_wk = grad_wk + dot(grad_ak, wk_ref[d], 1, 0)
-    over_core(1, grad_wk)
+    over_row(1, grad_wk)
 
     grad_aq = features_back(qf_ref[...], gqf_ref[...]).astype(BF16)
-    over_core(0, dot(grad_aq, q_ref[...], 1, 0))
+    over_row(0, dot(grad_aq, q_ref[...], 1, 0))
     student_ref[...] = estimate.T.astype(BF16)
     store = pltpu.make_async_copy(student_ref, student_hbm, store_sem.at[0])
     store.start()
-    over_y(1)
 
     final = code[:, count - 1 :]
     back = (code == final).astype(F32)
@@ -541,7 +532,6 @@
     gather_ref[0, z] = spread_ref[pl.ds(pl.multiple_of(z * share, share), share)]
 
     over_x(1)
-    over_y(0)
     z_ref[0, z] = over_seq(1).astype(BF16)
     here = z_ref.at[0, z]
     for i in range(1, n_z):
@@ -630,8 +620,7 @@
             VMEM((REACH, ADJ_ROWS, feat), BF16),
             VMEM((feat, count), BF16),
             VMEM((1, n_z, feat // n_z, count), BF16),
-            VMEM((2, 2, half, width), BF16),
-            VMEM((2, SIDE, half, width), BF16),
+            VMEM((2, 2 * SIDE, half, width), BF16),
             VMEM((2, SIDE, half, width), BF16),
             VMEM((1, n_z, half, width), BF16),
             dma((6,)),
@@ -651,10 +640,8 @@
             dma((REACH,)),
             dma((1, n_z - 1)),
             dma((1, n_z)),
-            dma((2, 1)),
-            dma((2, 2)),
-            dma((2, SIDE - 1)),
-            dma((2, SIDE)),
+            dma((2, 2 * SIDE - 1)),
+            dma((2, 2 * SIDE)),
             dma((2, SIDE - 1)),
             dma((2, SIDE)),
             dma((1, n_z - 1)),

time: 52.9 us -> 52.7 us (level)
  no operation moved by 1% of the time
where the time goes in v6:
time: 52.7 us; the launch traced here: 52.6 us
  Pallas kernels  52 us (99%)
  between operations  0.64 us (1%)
    pallas_call x1, Pallas kernels, fused(): pl.pallas_call(functools.partial(fused_kernel, n_seq, n_z), out_shape=(ja...  50.3 us
    pallas_call x1, Pallas kernels, publish(): pl.pallas_call(publish_kernel, out_shape=tuple((jax.ShapeDtypeStruct(r.sh...  1.72 us

profile of v6, /device:TPU:1, one launch (start us, length us, event | category | flops | bytes accessed | tf_op | source)
XLA Modules:
  0.0 52.6 jit_solution(14717263610165619214)
XLA Ops:
  0.6 50.3 %fused.1 = (bf16[1024,128]{1,0:T(8,128)(2,1)}, f32[64,128]{1,0:T(8,128)}, f32[64,128]{1,0:T(8,128)}, f32[16,1024]{1,0:T(8,128)}) custom-call(bf16[1024,128]{1,0:T(8,128)(2,1)} %bitcast.12, bf16[1024,128]{1,0:T(8,128)(2,1)} %k_hbm.1, bf16[1024,128]{1,0:T(8,128)(2,1)} %v_hbm.1, s32[1,1024]{1,0:T(1,128)} %bitcast.15, bf16[64,128]{1,0:T(8,128)(2,1)} %bitcast.13, ...), custom_call_target="tpu_custom_call" | custom-call | tf_op jit(solution)/shard_map/fused/pallas_call | solution.py:581
  50.9 1.7 %publish.1 = (bf16[1024,128]{1,0:T(8,128)(2,1)}, f32[64,128]{1,0:T(8,128)}, f32[64,128]{1,0:T(8,128)}, f32[16,1024]{1,0:T(8,128)}) custom-call(bf16[1024,128]{1,0:T(8,128)(2,1)} %get-tuple-element.12.refs_0_, f32[64,128]{1,0:T(8,128)} %get-tuple-element.13.refs_1_, f32[64,128]{1,0:T(8,128)} %get-tuple-element.14.refs_2_, f32[16,1024]{1,0:T(8,128)} %get-tuple-element.15.refs_3_), custom_call_target="tpu_custom_call" | custom-call | tf_op jit(solution)/shard_map/publish/pallas_call | solution.py:662
